TPU v7x, 32 devices: a 4x4x1 block of a 4x4x8 slice. The times are simulated.
32 devices in a mesh: dp: 1 (over z), tp: 4 (over y), sp: 8 (over x, core).
Axes of the slice: x: 4, y: 4, z: 1, core: 2. Of those that a mesh axis runs over, the one named last changes fastest.
The devices are a block of a 4x4x8 slice.
Arguments:
- hidden: bfloat16 [128, 4096], P('dp')
- seq_lens: int32 [128], P('dp')
- k_cache: bfloat16 [128, 8, 1024, 128], P('dp', 'tp', 'sp')
- v_cache: bfloat16 [128, 8, 1024, 128], P('dp', 'tp', 'sp')
- attn_norm: bfloat16 [4096], replicated
- w_q: bfloat16 [4096, 4096], P(None, 'tp')
- w_k: bfloat16 [4096, 1024], P(None, 'tp')
- w_v: bfloat16 [4096, 1024], P(None, 'tp')
- w_o: bfloat16 [4096, 4096], P('tp')
- mlp_norm: bfloat16 [4096], replicated
- w_gate: bfloat16 [4096, 14336], P(None, 'tp')
- w_up: bfloat16 [4096, 14336], P(None, 'tp')
- w_down: bfloat16 [14336, 4096], P('tp')
Outputs:
- output 1: bfloat16 [128, 4096], P('dp')
- output 2: bfloat16 [128, 8, 1024, 128], P('dp', 'tp', 'sp')
- output 3: bfloat16 [128, 8, 1024, 128], P('dp', 'tp', 'sp')
All inputs are finite; a program needn't handle non-finite values.
Results may differ from a plain program's by a relative error of at most 0.00515676.
Values sent between devices are 32-bit elements.
A program may use at most 768 MiB of HBM per device.

v0:
```python
import jax
import jax.numpy as jnp
from jax import lax
from jax.sharding import PartitionSpec as P

NORM_EPS = 1e-6
MASK_VALUE = -1e30


def rms_norm(values, gain):
    wide = values.astype(jnp.float32)
    scaled = wide * lax.rsqrt(jnp.mean(wide * wide, axis=-1, keepdims=True) + NORM_EPS)
    return (scaled * gain.astype(jnp.float32)).astype(jnp.bfloat16)


def project(normed, weight):
    return jnp.dot(normed, weight, preferred_element_type=jnp.float32).astype(jnp.bfloat16)


def solution(mesh):
    cache_spec = P('dp', 'tp', 'sp', None)
    row_spec = P('dp', None)
    col_spec = P(None, 'tp')
    inner_spec = P('tp', None)
    gain_spec = P(None)

    def local_step(hidden, seq_lens, k_cache, v_cache, attn_norm, w_q, w_k, w_v, w_o, mlp_norm, w_gate, w_up, w_down):
        batch_rows, groups, block_len, head_dim = k_cache.shape
        repeat = w_q.shape[1] // (groups * head_dim)
        normed = rms_norm(hidden, attn_norm)
        query = project(normed, w_q).reshape(batch_rows, groups, repeat, head_dim)
        k_new = project(normed, w_k).reshape(batch_rows, groups, 1, head_dim)
        v_new = project(normed, w_v).reshape(batch_rows, groups, 1, head_dim)
        positions = lax.axis_index('sp') * block_len + jnp.arange(block_len)
        new_slot = (positions[None, :] == seq_lens[:, None])[:, None, :, None]
        k_out = jnp.where(new_slot, k_new, k_cache)
        v_out = jnp.where(new_slot, v_new, v_cache)
        valid = (positions[None, :] <= seq_lens[:, None])[:, None, None, :]
        scores = jnp.einsum('bgrd,bgsd->bgrs', query, k_out, preferred_element_type=jnp.float32) * head_dim ** -0.5
        scores = jnp.where(valid, scores, MASK_VALUE)
        global_max = lax.pmax(jnp.max(scores, axis=-1, keepdims=True), 'sp')
        weights = jnp.where(valid, jnp.exp(scores - global_max), 0.0)
        local_sum = jnp.sum(weights, axis=-1, keepdims=True)
        local_mix = jnp.einsum('bgrs,bgsd->bgrd', weights.astype(jnp.bfloat16), v_out, preferred_element_type=jnp.float32)
        merged = lax.psum(jnp.concatenate([local_mix, local_sum], axis=-1), 'sp')
        attended = (merged[..., :head_dim] / merged[..., head_dim:]).astype(jnp.bfloat16).reshape(batch_rows, groups * repeat * head_dim)
        proj_part = jnp.dot(attended, w_o, preferred_element_type=jnp.float32)
        mid_hidden = (hidden.astype(jnp.float32) + lax.psum(proj_part, 'tp')).astype(jnp.bfloat16)
        normed_mid = rms_norm(mid_hidden, mlp_norm)
        gate_proj = jnp.dot(normed_mid, w_gate, preferred_element_type=jnp.float32)
        up_proj = jnp.dot(normed_mid, w_up, preferred_element_type=jnp.float32)
        activated = (jax.nn.silu(gate_proj) * up_proj).astype(jnp.bfloat16)
        down_part = jnp.dot(activated, w_down, preferred_element_type=jnp.float32)
        hidden_out = (mid_hidden.astype(jnp.float32) + lax.psum(down_part, 'tp')).astype(jnp.bfloat16)
        return hidden_out, k_out, v_out

    return jax.shard_map(local_step, mesh=mesh, in_specs=(row_spec, P('dp'), cache_spec, cache_spec, gain_spec, col_spec, col_spec, col_spec, inner_spec, gain_spec, col_spec, col_spec, inner_spec), out_specs=(row_spec, cache_spec, cache_spec), check_vma=False)
```

profile of v0, /device:TPU:97, one launch (start us, length us, event | category | flops | bytes accessed | tf_op | source)
XLA Modules:
  0.0 289.5 jit_solution(9976671300510736537)
XLA Ops:
  7.2 0.0 copy-start
  7.2 0.1 all-reduce.4.cloned.1.call-start
  7.3 1.7 fusion.2
  8.9 0.0 copy-start.3
  8.9 0.8 convert_element_type.45
  9.7 0.0 copy-done
  9.7 1.7 convolution_convert_fusion.2
  11.5 0.0 copy-done.3
  11.5 2.1 convolution_convert_fusion.1
  13.6 0.0 copy-start.6
  13.6 4.7 %convolution_convert_fusion = bf16[128,1024]{1,0:T(8,128)(2,1)S(1)} fusion(bf16[4096,1024]{1,0:T(8,128)(2,1)} %param.18, bf16[128,4096]{1,0:T(8,128)(2,1)S(1)} %copy-done.3, f32[4096]{0:T(1024)S(1)} %convert_element_type.45, f32[128]{0:T(128)S(1)} %add_rsqrt_fusion.1), kind=kOutput, calls=%fused_computation.26 | convolution fusion | flops 1075970048 | bytes 9716224 | tf_op jit(solution)/shard_map/dot_general | solution.py:17
  18.3 0.2 reshape.85
  18.5 0.0 copy-done.6
  18.5 0.1 broadcast_compare_fusion.1
  18.6 9.8 %broadcast_select_fusion = (bf16[128,2,128,128]{3,2,1,0:T(8,128)(2,1)}, bf16[128,2,128,128]{3,2,1,0:T(8,128)(2,1)S(1)}) fusion(bf16[128,2,128,128]{3,2,1,0:T(8,128)(2,1)} %param.16, pred[128,128]{1,0:T(8,128)(4,1)S(1)} %get-tuple-element.8, bf16[128,2,128]{2,1,0:T(2,128)(2,1)S(1)} %broadcast_in_dim.69, bf16[128,2,128,128]{3,2,1,0:T(8,128)(2,1)} %param.15, ...), kind=kLoop, calls=%fused_computation | loop fusion | flops 8388608 | bytes 33701888 | tf_op jit(solution)/shard_map/jit(_where)/select_n | solution.py:37
  28.4 0.0 copy-start.2
  28.4 4.7 %fusion.35 = (f32[128,2,4]{2,1,0:T(2,128)S(1)}, f32[128,2,4,128]{3,2,1,0:T(4,128)S(1)}) fusion(bf16[128,2,4,128]{3,2,1,0:T(4,128)(2,1)S(1)} %reshape.85, bf16[128,2,128,128]{3,2,1,0:T(8,128)(2,1)S(1)} %get-tuple-element.6, pred[128,128]{1,0:T(8,128)(4,1)S(1)} %get-tuple-element.7), kind=kOutput, calls=%fused_computation.48 | convolution fusion | flops 33946624 | bytes 9195520 | tf_op jit(solution)/shard_map/bgrd,bgsd->bgrs/dot_general | solution.py:39
  33.0 0.0 copy-done.2
  33.0 25.2 %pmax.7 = f32[128,2,4]{2,1,0:T(2,128)S(1)} all-reduce(f32[128,2,4]{2,1,0:T(2,128)S(1)} %get-tuple-element.9), channel_id=1, replica_groups=mesh['dp'=1,'tp'=4,'sp'=8] {'sp'}, use_global_device_ids=true, to_apply=%region_2.3 | all-reduce | flops 1024 | bytes 8192 | tf_op jit(solution)/shard_map/pmax | solution.py:41
  58.3 0.8 fusion.18
  59.1 5.7 %fusion.24 = f32[128,2,4,128]{3,2,1,0:T(4,128)S(1)} fusion(bf16[128,2,128,128]{3,2,1,0:T(8,128)(2,1)} %get-tuple-element.5, f32[128,2,4,128]{3,2,1,0:T(4,128)S(1)} %get-tuple-element.10, f32[128,2,4]{2,1,0:T(2,128)S(1)} %pmax.7, pred[128,128]{1,0:T(8,128)(4,1)S(1)} %get-tuple-element.7), kind=kOutput, calls=%fused_computation.37 | convolution fusion | flops 33947648 | bytes 9457664 | tf_op jit(solution)/shard_map/bgrs,bgsd->bgrd/dot_general | solution.py:44
  64.8 1.7 copy.20
  66.5 1.2 pad_maximum_fusion
  67.7 0.1 all-reduce.4.cloned.1.call-update
  67.8 0.2 all-reduce.6.cloned.1.call-start
  68.0 58.6 %all-reduce.4.cloned.1.call-done = f32[128,2,4,129]{3,2,1,0:T(4,128)} async-done(((f32[128,2,4,129]{3,2,1,0:T(4,128)}), f32[128,2,4,129]{3,2,1,0:T(4,128)}) %all-reduce.4.cloned.1.call-update) | async-done | bytes 528400 | tf_op jit(solution)/shard_map/psum | solution.py:45
  126.6 1.1 slice.9
  127.7 0.2 copy.21
  127.9 0.2 copy.22
  128.1 1.4 fusion.17
  129.5 0.2 reshape.86
  129.6 5.9 %fusion.36 = f32[128,4096]{1,0:T(8,128)} fusion(bf16[128,1024]{1,0:T(8,128)(2,1)S(1)} %reshape.86, bf16[1024,4096]{1,0:T(8,128)(2,1)} %param.21), kind=kOutput, calls=%fused_computation.49 | convolution fusion | flops 1073741824 | bytes 10747904 | tf_op jit(solution)/shard_map/dot_general | solution.py:47
  135.6 0.0 copy-start.5
  135.6 0.0 copy-start.4
  135.6 0.1 all-reduce.6.cloned.1.call-update
  135.7 0.1 all-reduce.8.cloned.1.call-start
  135.7 0.6 copy-done.5
  136.3 54.0 %all-reduce.6.cloned.1.call-done = f32[128,4096]{1,0:T(8,128)} async-done(((f32[128,4096]{1,0:T(8,128)}), f32[128,4096]{1,0:T(8,128)}) %all-reduce.6.cloned.1.call-update) | async-done | bytes 2097168 | tf_op jit(solution)/shard_map/psum | solution.py:48
  190.3 0.0 copy-done.4
  190.3 2.0 fusion.6
  192.3 11.5 %fusion.22 = f32[128,3584]{1,0:T(8,128)S(1)} fusion(bf16[4096,3584]{1,0:T(8,128)(2,1)} %param.23, bf16[128,4096]{1,0:T(8,128)(2,1)S(1)} %get-tuple-element.4, f32[4096]{0:T(1024)S(1)} %convert_element_type.54, f32[128]{0:T(128)S(1)} %add_rsqrt_fusion), kind=kOutput, calls=%fused_computation.36 | convolution fusion | flops 3760193536 | bytes 32260608 | tf_op jit(solution)/shard_map/dot_general | solution.py:50
  203.9 22.9 %fusion.1 = f32[128,4096]{1,0:T(8,128)} fusion(bf16[3584,4096]{1,0:T(8,128)(2,1)} %param.25, bf16[4096,3584]{1,0:T(8,128)(2,1)} %param.24, f32[128,3584]{1,0:T(8,128)S(1)} %fusion.22, bf16[128,4096]{1,0:T(8,128)(2,1)S(1)} %get-tuple-element.4, f32[4096]{0:T(1024)S(1)} %convert_element_type.54, f32[128]{0:T(128)S(1)} %add_rsqrt_fusion), kind=kOutput, calls=%fused_computation.4 | convolution fusion | flops 7521042432 | bytes 63717888 | tf_op jit(solution)/shard_map/dot_general | solution.py:53
  226.8 0.1 all-reduce.8.cloned.1.call-update
  226.8 0.0 copy-start.1
  226.8 53.3 %all-reduce.8.cloned.1.call-done = f32[128,4096]{1,0:T(8,128)} async-done(((f32[128,4096]{1,0:T(8,128)}), f32[128,4096]{1,0:T(8,128)}) %all-reduce.8.cloned.1.call-update) | async-done | bytes 2097168 | tf_op jit(solution)/shard_map/psum | solution.py:54
  280.2 2.8 fusion.9
  282.9 0.0 copy-done.1
  (6 shorter events, 0.1 us)
Async XLA Ops:
  7.2 2.6 copy-start
  7.2 119.4 %all-reduce.4.cloned.1.call-start = ((), (), s32[]{:S(2)}) async-start(), calls=%async_computation | async-start | bytes 2097152 | tf_op jit(solution)/shard_map/psum | solution.py:45
  8.9 2.6 copy-start.3
  13.6 4.9 %copy-start.6 = (s32[128]{0:T(128)S(1)}, s32[128]{0:T(128)}, u32[]{:S(2)}) copy-start(s32[128]{0:T(128)} %param.14) | copy-start | bytes 1540
  28.4 4.7 %copy-start.2 = (bf16[128,2,128,128]{3,2,1,0:T(8,128)(2,1)}, bf16[128,2,128,128]{3,2,1,0:T(8,128)(2,1)S(1)}, u32[]{:S(2)}) copy-start(bf16[128,2,128,128]{3,2,1,0:T(8,128)(2,1)S(1)} %get-tuple-element.6) | copy-start | bytes 25165828
  67.8 122.6 %all-reduce.6.cloned.1.call-start = ((), (), s32[]{:S(2)}) async-start(), calls=%async_computation.1 | async-start | bytes 4194304 | tf_op jit(solution)/shard_map/psum | solution.py:48
  135.6 0.7 copy-start.5
  135.6 54.8 %copy-start.4 = (bf16[128,4096]{1,0:T(8,128)(2,1)S(1)}, bf16[128,4096]{1,0:T(8,128)(2,1)}, u32[]{:S(2)}) copy-start(bf16[128,4096]{1,0:T(8,128)(2,1)} %param.13) | copy-start | bytes 3145732
  135.7 144.5 %all-reduce.8.cloned.1.call-start = ((), (), s32[]{:S(2)}) async-start(), calls=%async_computation.2 | async-start | bytes 4194304 | tf_op jit(solution)/shard_map/psum | solution.py:54
  226.8 56.1 %copy-start.1 = (bf16[4096,256]{1,0:T(8,128)(2,1)S(1)}, bf16[4096,256]{1,0:T(8,128)(2,1)}, u32[]{:S(2)}) copy-start(bf16[4096,256]{1,0:T(8,128)(2,1)} %param.19) | copy-start | bytes 6291460
Sparse Core Ops, SparseCore 0:
  67.9 58.6 all-reduce.3
  135.8 54.5 all-reduce.5
  226.9 53.1 all-reduce.7
where the time goes:
time: 290 us; the launch traced here: 289 us
  waiting for transfers between devices  166 us (57%)
  matrix products  59.2 us (20%)
  blocking collectives  25.2 us (9%)
  other arithmetic  20.5 us (7%)
  between operations  13.9 us (5%)
  local copies, waits for them, and re-layouts  4.14 us (1%)
    psum x1, waiting for transfers between devices, local_step(): merged = lax.psum(jnp.concatenate([local_mix, local_sum], axis=-1), 'sp')  58.6 us
    psum x1, waiting for transfers between devices, local_step(): lax.psum(proj_part, 'tp')  54 us
    psum x1, waiting for transfers between devices, local_step(): lax.psum(down_part, 'tp')  53.3 us
    pmax x1, blocking collectives, local_step(): global_max = lax.pmax(jnp.max(scores, axis=-1, keepdims=True), 'sp')  25.2 us
    dot_general x1, matrix products, local_step(): down_part = jnp.dot(activated, w_down, preferred_element_type=jnp.float32)  22.9 us
    dot_general x1, matrix products, local_step(): gate_proj = jnp.dot(normed_mid, w_gate, preferred_element_type=jnp.float32)  11.5 us
    select_n x1, other arithmetic, local_step(): v_out = jnp.where(new_slot, v_new, v_cache)  9.76 us
    dot_general x3, matrix products, project(): jnp.dot(normed, weight, preferred_element_type=jnp.float32)  8.48 us
  transfers between devices with their start and end apart: 3, of which 3 were waited for; matrix products, arithmetic and copies ran while one was open for 0% of the time, Pallas kernels for 0%

commit v1 on v0

v1 whole, which is shorter than its diff:
```python
import functools
import jax
import jax.numpy as jnp
from jax import lax
from jax.experimental import pallas as pl
from jax.experimental.pallas import tpu as pltpu
from jax.sharding import PartitionSpec as P

NORM_EPS = 1e-6
MASK_VALUE = -3e38
F32 = jnp.float32
BF16 = jnp.bfloat16
MESH = pl.DeviceIdType.MESH
CORES = 2
COLS = 256
VMEM_LIMIT = 66_000_000


def dot32(a, b):
    return jnp.dot(a, b, preferred_element_type=F32)


def attn_kernel(lens, hid, gain, wq, wk, wv, kc, vc, o_out, st_out, k_out, v_out,
                hbuf, gbuf, ubuf, wbuf, qbuf, knew, vnew, kbuf, vbuf, obuf,
                hsem, wsem, kin, vin, kos, vos):
    rows, groups, blk, dim = kc.shape
    heads = wq.shape[1] // dim
    rep = heads // groups
    nq = wq.shape[1] // COLS
    nkv = wk.shape[1] // COLS
    nchunk = kin.shape[0]
    crow = rows // nchunk
    base = lax.axis_index('sp') * blk

    def load(i):
        r = pl.ds(i * crow, crow)
        return (pltpu.make_async_copy(kc.at[r], kbuf.at[r], kin.at[i]),
                pltpu.make_async_copy(vc.at[r], vbuf.at[r], vin.at[i]))

    def store(i):
        r = pl.ds(i * crow, crow)
        return (pltpu.make_async_copy(kbuf.at[r], k_out.at[r], kos.at[i]),
                pltpu.make_async_copy(vbuf.at[r], v_out.at[r], vos.at[i]))

    hcopy = pltpu.make_async_copy(hid, hbuf, hsem.at[0])
    gcopy = pltpu.make_async_copy(gain, gbuf, hsem.at[1])
    hcopy.start()
    gcopy.start()
    wcopies = []
    for src, n in ((wq, nq), (wk, nkv), (wv, nkv)):
        for j in range(n):
            t = len(wcopies)
            wcopies.append(pltpu.make_async_copy(src.at[:, pl.ds(j * COLS, COLS)], wbuf.at[t], wsem.at[t]))
    for cp in wcopies:
        cp.start()
    for i in range(2):
        for cp in load(i):
            cp.start()
    hcopy.wait()
    gcopy.wait()
    g = gbuf[...].astype(F32)
    for r in range(0, rows, 16):
        wide = hbuf[r:r + 16, :].astype(F32)
        inv = lax.rsqrt(jnp.mean(wide * wide, axis=-1, keepdims=True) + NORM_EPS)
        ubuf[r:r + 16, :] = (wide * inv * g).astype(BF16)

    issued = 2
    for t, cp in enumerate(wcopies):
        cp.wait()
        if issued < nchunk:
            for c2 in load(issued):
                c2.start()
            issued += 1
        res = dot32(ubuf[...], wbuf[t])
        per = COLS // dim
        for s in range(per):
            part = res[:, s * dim:(s + 1) * dim]
            if t < nq:
                qbuf[pl.ds(t * per + s, rows, stride=heads), :] = part
            elif t < nq + nkv:
                knew[(t - nq) * per + s] = part
            else:
                vnew[(t - nq - nkv) * per + s] = part
    while issued < nchunk:
        for c2 in load(issued):
            c2.start()
        issued += 1

    pair = 2 * heads
    row_id = lax.broadcasted_iota(jnp.int32, (pair, blk), 0)
    lane_id = lax.broadcasted_iota(jnp.int32, (pair, blk), 1)
    first = row_id < heads
    low = (row_id % heads) < rep
    stat_lane = lax.broadcasted_iota(jnp.int32, (heads, rows), 1)
    tile_row = lax.broadcasted_iota(jnp.int32, (16, dim), 0)
    scale = dim ** -0.5

    def chunk(i, carry):
        m_acc, l_acc = carry
        for cp in load(i):
            cp.wait()

        def patch(r, _):
            b = i * crow + r
            off = lens[b] - base
            hit = jnp.logical_and(off >= 0, off < blk)
            offc = jnp.clip(off, 0, blk - 1)
            t16 = pl.multiple_of((offc // 16) * 16, 16)
            want = jnp.where(hit, offc - t16, -1)
            mask = tile_row == want
            for gi in range(groups):
                kt = kbuf[b, gi, pl.ds(t16, 16), :]
                kbuf[b, gi, pl.ds(t16, 16), :] = jnp.where(mask, jnp.broadcast_to(knew[gi, pl.ds(b, 1), :], (16, dim)).astype(BF16), kt)
                vt = vbuf[b, gi, pl.ds(t16, 16), :]
                vbuf[b, gi, pl.ds(t16, 16), :] = jnp.where(mask, jnp.broadcast_to(vnew[gi, pl.ds(b, 1), :], (16, dim)).astype(BF16), vt)
            return 0

        lax.fori_loop(0, crow, patch, 0)
        for cp in store(i):
            cp.start()

        for r in range(0, crow, 2):
            b = i * crow + r
            q16 = qbuf[pl.ds(pl.multiple_of(b * heads, pair), pair), :]
            lhs = jnp.concatenate([jnp.where(first, q16, 0.0), jnp.where(first, 0.0, q16)], axis=1).astype(BF16)
            keys = jnp.concatenate([kbuf[b].reshape(groups * blk, dim), kbuf[b + 1].reshape(groups * blk, dim)], axis=1)
            sc = lax.dot_general(lhs, keys, (((1,), (1,)), ((), ())), preferred_element_type=F32)
            s = jnp.where(low, sc[:, :blk], sc[:, blk:]) * scale
            limit = jnp.where(first, lens[b] - base, lens[b + 1] - base)
            valid = lane_id <= limit
            s = jnp.where(valid, s, MASK_VALUE)
            m = jnp.max(s, axis=1, keepdims=True)
            p = jnp.where(valid, jnp.exp(s - m), 0.0)
            tot = jnp.sum(p, axis=1, keepdims=True)
            pcat = jnp.concatenate([jnp.where(low, p, 0.0), jnp.where(low, 0.0, p)], axis=1).astype(BF16)
            vals = jnp.concatenate([vbuf[b].reshape(groups * blk, dim), vbuf[b + 1].reshape(groups * blk, dim)], axis=1)
            mix = dot32(pcat, vals)
            obuf[pl.ds(pl.multiple_of(b * heads, pair), heads), :] = mix[:heads, :dim]
            obuf[pl.ds(pl.multiple_of(b * heads + heads, heads), heads), :] = mix[heads:, dim:]
            m_acc = jnp.where(stat_lane == b, m[:heads], jnp.where(stat_lane == b + 1, m[heads:], m_acc))
            l_acc = jnp.where(stat_lane == b, tot[:heads], jnp.where(stat_lane == b + 1, tot[heads:], l_acc))
        return m_acc, l_acc

    zero = jnp.zeros((heads, rows), F32)
    m_acc, l_acc = lax.fori_loop(0, nchunk, chunk, (zero, zero))
    half = heads // CORES
    for ci in range(CORES):
        st_out[ci] = jnp.concatenate([m_acc[ci * half:(ci + 1) * half], l_acc[ci * half:(ci + 1) * half]], axis=0)
    for h in range(heads):
        o_out[h] = obuf[pl.ds(h, rows, stride=heads), :]

    def drain(i, _):
        for cp in store(i):
            cp.wait()
        return 0

    lax.fori_loop(0, nchunk, drain, 0)


def attention(hidden, seq_lens, k_cache, v_cache, gain, w_q, w_k, w_v):
    rows, groups, blk, dim = k_cache.shape
    heads = w_q.shape[1] // dim
    width = w_q.shape[0]
    nw = (w_q.shape[1] + w_k.shape[1] + w_v.shape[1]) // COLS
    nchunk = 8
    any_spec = pl.BlockSpec(memory_space=pl.ANY)
    vm = pl.BlockSpec(memory_space=pltpu.VMEM)
    return pl.pallas_call(
        attn_kernel,
        name='block_attention',
        out_shape=(jax.ShapeDtypeStruct((heads, rows, dim), F32),
                   jax.ShapeDtypeStruct((CORES, heads, rows), F32),
                   jax.ShapeDtypeStruct(k_cache.shape, BF16),
                   jax.ShapeDtypeStruct(v_cache.shape, BF16)),
        in_specs=[pl.BlockSpec(memory_space=pltpu.SMEM)] + [any_spec] * 7,
        out_specs=(vm, vm, any_spec, any_spec),
        scratch_shapes=[
            pltpu.VMEM((rows, width), BF16),
            pltpu.VMEM((1, width), BF16),
            pltpu.VMEM((rows, width), BF16),
            pltpu.VMEM((nw, width, COLS), BF16),
            pltpu.VMEM((rows * heads, dim), F32),
            pltpu.VMEM((groups, rows, dim), F32),
            pltpu.VMEM((groups, rows, dim), F32),
            pltpu.VMEM(k_cache.shape, BF16),
            pltpu.VMEM(v_cache.shape, BF16),
            pltpu.VMEM((rows * heads, dim), F32),
            pltpu.SemaphoreType.DMA((2,)),
            pltpu.SemaphoreType.DMA((nw,)),
            pltpu.SemaphoreType.DMA((nchunk,)),
            pltpu.SemaphoreType.DMA((nchunk,)),
            pltpu.SemaphoreType.DMA((nchunk,)),
            pltpu.SemaphoreType.DMA((nchunk,)),
        ],
        compiler_params=pltpu.CompilerParams(vmem_limit_bytes=VMEM_LIMIT),
    )(seq_lens, hidden, gain.reshape(1, width), w_q, w_k, w_v, k_cache, v_cache)


def mlp_kernel(nx, ny, hid, o_in, st_in, gain, wo, wg, wu, wd, out,
               wo_b, wg_b, wu_b, wd_b, hid_b, gain_b, o_b, st_b, po_b, pst_b, oc_b, cst_b, xo_b, xst_b, tst_b,
               att_b, pw_b, rw_b, mid_b, u2_b, act_b, ab_b, pd_b, rd_b, fin_b,
               lsem, wsem, ds_s, ds_r, xs_s, xs_r, as_s, as_r, ws_s, ws_r, ms_s, ms_r, cs_s, cs_r, dn_s, dn_r, fs_s, fs_r, fp_s, fp_r):
    sp = lax.axis_index('sp')
    y = lax.axis_index('tp')
    x = sp // CORES
    c = sp % CORES
    oc = 1 - c
    half_h, rows, dim = po_b.shape
    xr = rows // nx
    width = gain.shape[1]
    hw = width // CORES
    cw = hw // ny
    partner = {'tp': y, 'sp': x * CORES + oc}

    def peer(yy, xx):
        return {'tp': yy, 'sp': xx * CORES + c}

    def rcopy(src, dst, ssem, rsem, dev):
        return pltpu.make_async_remote_copy(src_ref=src, dst_ref=dst, send_sem=ssem, recv_sem=rsem, device_id=dev, device_id_type=MESH)

    def cols(i, n):
        return pl.ds(pl.multiple_of(i * n, n), n)

    loads = [
        pltpu.make_async_copy(o_in, o_b, lsem.at[0]),
        pltpu.make_async_copy(st_in, st_b, lsem.at[1]),
        pltpu.make_async_copy(hid.at[pl.ds(x * xr, xr), pl.ds(pl.multiple_of(c * hw + y * cw, cw), cw)], hid_b, lsem.at[2]),
        pltpu.make_async_copy(gain, gain_b, lsem.at[3]),
    ]
    for cp in loads:
        cp.start()
    inner = wg_b.shape[1]
    w_loads = [
        pltpu.make_async_copy(wo.at[:, cols(c, hw)], wo_b, wsem.at[0]),
        pltpu.make_async_copy(wg.at[:, cols(c, inner)], wg_b, wsem.at[1]),
        pltpu.make_async_copy(wu.at[:, cols(c, inner)], wu_b, wsem.at[2]),
        pltpu.make_async_copy(wd.at[:, cols(c, hw)], wd_b, wsem.at[3]),
    ]
    for cp in w_loads:
        cp.start()

    barrier = pltpu.get_barrier_semaphore()
    pl.semaphore_signal(barrier, inc=1, device_id=partner, device_id_type=MESH)
    for k in range(1, nx):
        pl.semaphore_signal(barrier, inc=1, device_id=peer(y, (x + k) % nx), device_id_type=MESH)
    for k in range(1, ny):
        pl.semaphore_signal(barrier, inc=1, device_id=peer((y + k) % ny, x), device_id_type=MESH)
    for cp in loads:
        cp.wait()
    pl.semaphore_wait(barrier, 1 + (nx - 1) + (ny - 1))

    d2d = [rcopy(o_b.at[pl.ds(half_h * oc, half_h)], po_b, ds_s.at[0], ds_r.at[0], partner),
           rcopy(st_b.at[oc], pst_b, ds_s.at[1], ds_r.at[1], partner)]
    for cp in d2d:
        cp.start()
    for cp in d2d:
        cp.wait()
    s0 = st_b[c]
    s1 = pst_b[...]
    m0, l0, m1, l1 = s0[:half_h], s0[half_h:], s1[:half_h], s1[half_h:]
    mm = jnp.maximum(m0, m1)
    a0, a1 = jnp.exp(m0 - mm), jnp.exp(m1 - mm)
    cst_b[...] = jnp.concatenate([mm, a0 * l0 + a1 * l1], axis=0)
    tr = jnp.concatenate([a0, a1], axis=0).T
    for h in range(half_h):
        oc_b[h] = o_b[half_h * c + h] * tr[:, h:h + 1] + po_b[h] * tr[:, half_h + h:half_h + h + 1]

    sends = []
    for k in range(1, nx):
        xx = (x + k) % nx
        sends.append(rcopy(cst_b, xst_b.at[x], xs_s.at[k - 1, 0], xs_r.at[x, 0], peer(y, xx)))
        sends.append(rcopy(oc_b.at[:, pl.ds(xx * xr, xr), :], xo_b.at[x], xs_s.at[k - 1, 1], xs_r.at[x, 1], peer(y, xx)))
    for cp in sends:
        cp.start()
    tst_b[0] = cst_b[...].T
    for k in range(1, nx):
        xx = (x + k) % nx
        rcopy(cst_b, xst_b.at[xx], xs_s.at[k - 1, 0], xs_r.at[xx, 0], peer(y, xx)).wait_recv()
        tst_b[k] = xst_b[xx].T
    stats = [tst_b[k, pl.ds(x * xr, xr), :] for k in range(nx)]
    mm = stats[0][:, :half_h]
    for k in range(1, nx):
        mm = jnp.maximum(mm, stats[k][:, :half_h])
    alphas = [jnp.exp(st[:, :half_h] - mm) for st in stats]
    total = alphas[0] * stats[0][:, half_h:]
    for k in range(1, nx):
        total = total + alphas[k] * stats[k][:, half_h:]
    for k in range(1, nx):
        xx = (x + k) % nx
        rcopy(oc_b.at[:, pl.ds(xx * xr, xr), :], xo_b.at[xx], xs_s.at[k - 1, 1], xs_r.at[xx, 1], peer(y, xx)).wait_recv()
    for h in range(half_h):
        acc = oc_b[h, pl.ds(x * xr, xr), :] * alphas[0][:, h:h + 1]
        for k in range(1, nx):
            acc = acc + xo_b[(x + k) % nx, h] * alphas[k][:, h:h + 1]
        att_b[c, :, h * dim:(h + 1) * dim] = (acc / total[:, h:h + 1]).astype(BF16).astype(F32)
    swap = rcopy(att_b.at[c], att_b.at[c], as_s.at[0], as_r.at[0], partner)
    swap.start()
    for cp in sends:
        cp.wait_send()
    rcopy(att_b.at[oc], att_b.at[oc], as_s.at[0], as_r.at[0], partner).wait_recv()
    swap.wait_send()

    def reduce_y(lhs_of, w_b, send_b, recv_b, s_sem, r_sem):
        lhs = lhs_of()
        started = []
        for k in [2, 1, 3, 0] if ny == 4 else list(range(1, ny)) + [0]:
            yy = (y + k) % ny
            send_b[yy] = dot32(lhs, w_b[:, cols(yy, cw)])
            if k:
                cp = rcopy(send_b.at[yy], recv_b.at[y], s_sem.at[k], r_sem.at[y], peer(yy, x))
                cp.start()
                started.append(cp)
        total = send_b[y]
        for k in range(1, ny):
            yy = (y + k) % ny
            rcopy(send_b.at[yy], recv_b.at[yy], s_sem.at[k], r_sem.at[yy], peer(yy, x)).wait_recv()
            total = total + recv_b[yy]
        for cp in started:
            cp.wait_send()
        return total

    w_loads[0].wait()
    total = reduce_y(lambda: jnp.concatenate([att_b[0], att_b[1]], axis=1).astype(BF16), wo_b, pw_b, rw_b, ws_s, ws_r)
    mid_b[c, y] = (hid_b[...].astype(F32) + total).astype(BF16).astype(F32)

    started = [rcopy(mid_b.at[c, y], mid_b.at[c, y], cs_s.at[0], cs_r.at[y], partner)]
    for k in range(1, ny):
        yy = (y + k) % ny
        started.append(rcopy(mid_b.at[c, y], mid_b.at[c, y], ms_s.at[k], ms_r.at[y], peer(yy, x)))
    for cp in started:
        cp.start()
    for k in range(1, ny):
        yy = (y + k) % ny
        rcopy(mid_b.at[c, yy], mid_b.at[c, yy], ms_s.at[k], ms_r.at[yy], peer(yy, x)).wait_recv()
        cp = rcopy(mid_b.at[c, yy], mid_b.at[c, yy], cs_s.at[k], cs_r.at[yy], partner)
        cp.start()
        started.append(cp)
    for k in range(ny):
        yy = (y + k) % ny
        rcopy(mid_b.at[oc, yy], mid_b.at[oc, yy], cs_s.at[k], cs_r.at[yy], partner).wait_recv()
    sq = jnp.zeros((xr, 1), F32)
    for ci in range(CORES):
        for yi in range(ny):
            v = mid_b[ci, yi]
            sq = sq + jnp.sum(v * v, axis=-1, keepdims=True)
    inv = lax.rsqrt(sq / width + NORM_EPS)
    for ci in range(CORES):
        for yi in range(ny):
            o = ci * hw + yi * cw
            u2_b[:, o:o + cw] = (mid_b[ci, yi] * inv * gain_b[:, o:o + cw].astype(F32)).astype(BF16)
    for cp in started:
        cp.wait_send()

    w_loads[1].wait()
    w_loads[2].wait()
    steps = inner // COLS

    def gate_up(j, _):
        lhs = u2_b[...]
        gp = dot32(lhs, wg_b[:, cols(j, COLS)])
        up = dot32(lhs, wu_b[:, cols(j, COLS)])
        act_b[c, j] = (gp * jax.nn.sigmoid(gp) * up).astype(BF16).astype(F32)
        rcopy(act_b.at[c, j], act_b.at[c, j], dn_s.at[j], dn_r.at[j], partner).start()
        return 0

    lax.fori_loop(0, steps, gate_up, 0)

    def take(j, _):
        rcopy(act_b.at[oc, j], act_b.at[oc, j], dn_s.at[j], dn_r.at[j], partner).wait()
        for ci in range(CORES):
            ab_b[:, pl.ds(pl.multiple_of(ci * inner + j * COLS, COLS), COLS)] = act_b[ci, j].astype(BF16)
        return 0

    lax.fori_loop(0, steps, take, 0)
    w_loads[3].wait()
    total = reduce_y(lambda: ab_b[...], wd_b, pd_b, rd_b, fs_s, fs_r)
    fin_b[x, y, c] = (mid_b[c, y] + total).astype(BF16).astype(F32)

    def slot(yy, xx):
        return fin_b.at[xx, yy, c]

    def place(k1, k2):
        return (y + k1 * oc + k2 * c) % ny, (x + k1 * c + k2 * oc) % nx

    started = []

    def spread(k1):
        sy, sx = place(k1, 0)
        for k2 in [2, 1, 3] if nx == 4 else range(1, nx):
            ty, tx = place(0, k2)
            cp = rcopy(slot(sy, sx), slot(sy, sx), fp_s.at[k1, k2], fp_r.at[sx, sy, c], peer(ty, tx))
            cp.start()
            started.append(cp)
        cp = rcopy(slot(sy, sx), slot(sy, sx), fp_s.at[k1, 0], fp_r.at[sx, sy, c], partner)
        cp.start()
        started.append(cp)

    for k1 in [2, 1, 3] if ny == 4 else range(1, ny):
        ty, tx = place(k1, 0)
        cp = rcopy(slot(y, x), slot(y, x), fp_s.at[0, nx + k1], fp_r.at[x, y, c], peer(ty, tx))
        cp.start()
        started.append(cp)
    spread(0)

    def arrived(yy, xx, ci):
        return rcopy(fin_b.at[xx, yy, ci], fin_b.at[xx, yy, ci], fp_s.at[0, 0], fp_r.at[xx, yy, ci], partner)

    for k1 in [1, 3, 2] if ny == 4 else range(1, ny):
        sy, sx = place(k1, 0)
        arrived(sy, sx, c).wait_recv()
        spread(k1)
    for k1 in [0, 1, 3, 2] if ny == 4 else range(ny):
        for k2 in [1, 3, 2] if nx == 4 else range(1, nx):
            sy, sx = place(k1, k2)
            arrived(sy, sx, c).wait_recv()
            cp = rcopy(slot(sy, sx), slot(sy, sx), fp_s.at[k1, nx + ny + k2], fp_r.at[sx, sy, c], partner)
            cp.start()
            started.append(cp)
    for xi in range(nx):
        for yi in range(ny):
            arrived(yi, xi, oc).wait_recv()
    for xi in range(nx):
        for yi in range(ny):
            for ci in range(CORES):
                o = ci * hw + yi * cw
                out[xi * xr:(xi + 1) * xr, o:o + cw] = fin_b[xi, yi, ci].astype(BF16)
    for cp in started:
        cp.wait_send()


def mlp(mesh, hidden, o_part, stats, gain, w_o, w_gate, w_up, w_down):
    rows, width = hidden.shape
    heads, _, dim = o_part.shape
    half_h = heads // CORES
    nx = mesh.shape['sp'] // CORES
    ny = mesh.shape['tp']
    xr = rows // nx
    hw = width // CORES
    cw = hw // ny
    inner = w_gate.shape[1] // CORES
    steps = inner // COLS
    any_spec = pl.BlockSpec(memory_space=pl.ANY)
    dma = pltpu.SemaphoreType.DMA
    return pl.pallas_call(
        functools.partial(mlp_kernel, nx, ny),
        name='exchange_mlp',
        out_shape=jax.ShapeDtypeStruct(hidden.shape, BF16),
        in_specs=[any_spec] * 8,
        out_specs=pl.BlockSpec(memory_space=pltpu.VMEM),
        scratch_shapes=[
            pltpu.VMEM((w_o.shape[0], hw), BF16),
            pltpu.VMEM((width, inner), BF16),
            pltpu.VMEM((width, inner), BF16),
            pltpu.VMEM((w_down.shape[0], hw), BF16),
            pltpu.VMEM((xr, cw), BF16),
            pltpu.VMEM((1, width), BF16),
            pltpu.VMEM((heads, rows, dim), F32),
            pltpu.VMEM((CORES, heads, rows), F32),
            pltpu.VMEM((half_h, rows, dim), F32),
            pltpu.VMEM((heads, rows), F32),
            pltpu.VMEM((half_h, rows, dim), F32),
            pltpu.VMEM((heads, rows), F32),
            pltpu.VMEM((nx, half_h, xr, dim), F32),
            pltpu.VMEM((nx, heads, rows), F32),
            pltpu.VMEM((nx, rows, heads), F32),
            pltpu.VMEM((CORES, xr, half_h * dim), F32),
            pltpu.VMEM((ny, xr, cw), F32),
            pltpu.VMEM((ny, xr, cw), F32),
            pltpu.VMEM((CORES, ny, xr, cw), F32),
            pltpu.VMEM((xr, width), BF16),
            pltpu.VMEM((CORES, steps, xr, COLS), F32),
            pltpu.VMEM((xr, CORES * inner), BF16),
            pltpu.VMEM((ny, xr, cw), F32),
            pltpu.VMEM((ny, xr, cw), F32),
            pltpu.VMEM((nx, ny, CORES, xr, cw), F32),
            dma((4,)), dma((4,)),
            dma((2,)), dma((2,)),
            dma((nx, 2)), dma((nx, 2)),
            dma((1,)), dma((1,)),
            dma((ny,)), dma((ny,)),
            dma((ny,)), dma((ny,)),
            dma((ny,)), dma((ny,)),
            dma((steps,)), dma((steps,)),
            dma((ny,)), dma((ny,)),
            dma((ny, 2 * nx + ny)), dma((nx, ny, CORES)),
        ],
        compiler_params=pltpu.CompilerParams(vmem_limit_bytes=VMEM_LIMIT, collective_id=0, has_side_effects=True),
    )(hidden, o_part, stats, gain.reshape(1, width), w_o, w_gate, w_up, w_down)


def solution(mesh):
    cache_spec = P('dp', 'tp', 'sp', None)
    row_spec = P('dp', None)
    col_spec = P(None, 'tp')
    inner_spec = P('tp', None)
    gain_spec = P(None)

    def local_step(hidden, seq_lens, k_cache, v_cache, attn_norm, w_q, w_k, w_v, w_o, mlp_norm, w_gate, w_up, w_down):
        o_part, stats, k_out, v_out = attention(hidden, seq_lens, k_cache, v_cache, attn_norm, w_q, w_k, w_v)
        hidden_out = mlp(mesh, hidden, o_part, stats, mlp_norm, w_o, w_gate, w_up, w_down)
        return hidden_out, k_out, v_out

    return jax.shard_map(local_step, mesh=mesh, in_specs=(row_spec, P('dp'), cache_spec, cache_spec, gain_spec, col_spec, col_spec, col_spec, inner_spec, gain_spec, col_spec, col_spec, inner_spec), out_specs=(row_spec, cache_spec, cache_spec), check_vma=False)
```

time: 290 us -> 104 us (0.36)
  waiting for transfers between devices: 166 us -> 0 us
  Pallas kernels: 0 us -> 98.1 us
  matrix products: 59.2 us -> 0 us
  blocking collectives: 25.2 us -> 0 us
  other arithmetic: 20.5 us -> 0 us
  between operations: 13.9 us -> 0.65 us
    psum x3 -> x0, waiting for transfers between devices: 166 us -> none  [the longest x1 58.6 us: local_step(): merged = lax.psum(jnp.concatenate([local_mix, local_sum], axis=-1), 'sp')]
    pallas_call x0 -> x2, Pallas kernels: none -> 98.1 us  [the longest x1 65.2 us: mlp(): pl.pallas_call(functools.partial(mlp_kernel, nx, ny), name='exchange_mlp'...]
    dot_general x8 -> x0, matrix products: 59.2 us -> none  [the longest x1 22.9 us: local_step(): down_part = jnp.dot(activated, w_down, preferred_element_type=jnp.float32)]
    pmax x1 -> x0, blocking collectives: 25.2 us -> none  [local_step(): global_max = lax.pmax(jnp.max(scores, axis=-1, keepdims=True), 'sp')]
    select_n x1 -> x0, other arithmetic: 9.76 us -> none  [local_step(): v_out = jnp.where(new_slot, v_new, v_cache)]
    convert_element_type x4 -> x0, other arithmetic: 4.95 us -> none  [the longest x1 2.77 us: local_step(): (mid_hidden.astype(jnp.float32) + lax.psum(down_part, 'tp')).astype(jnp.b...]
    reduce_sum x3 -> x0, other arithmetic: 4.43 us -> none  [the longest x2 3.64 us: rms_norm(): jnp.mean(wide * wide, axis=-1, keepdims=True) + NORM_EPS]
  transfers between devices with their start and end apart: 3 -> 0, of which waited for: 3 -> 0; matrix products, arithmetic and copies ran while one was open for 0% -> 0% of each run, Pallas kernels for 0% -> 0%
where the time goes in v1:
time: 104 us
  Pallas kernels  98.1 us (94%)
  local copies, waits for them, and re-layouts  4.9 us (5%)
    pallas_call x1, Pallas kernels, mlp(): pl.pallas_call(functools.partial(mlp_kernel, nx, ny), name='exchange_mlp'...  65.2 us
    pallas_call x1, Pallas kernels, attention(): pl.pallas_call(attn_kernel, name='block_attention', out_shape=(jax.ShapeD...  32.9 us
    unnamed x1, local copies, waits for them, and re-layouts  2.29 us

profile of v1, /device:TPU:97, one launch (start us, length us, event | category | flops | bytes accessed | tf_op | source)
XLA Modules:
  0.0 103.6 jit_solution(12431869693247017094)
XLA Ops:
  0.6 1.3 %reshape.12.gain = bf16[1,4096]{1,0:T(2,128)(2,1)} reshape(bf16[4096]{0:T(1024)(128)(2,1)} %param.17) | data formatting | bytes 16384 | tf_op jit(solution)/shard_map/reshape | solution.py:196
  1.9 1.3 %reshape.13.gain = bf16[1,4096]{1,0:T(2,128)(2,1)} reshape(bf16[4096]{0:T(1024)(128)(2,1)} %param.22) | data formatting | bytes 16384 | tf_op jit(solution)/shard_map/reshape | solution.py:488
  3.2 32.9 %block_attention.1 = (f32[8,128,128]{2,1,0:T(8,128)}, f32[2,8,128]{2,1,0:T(8,128)}, bf16[128,2,128,128]{3,2,1,0:T(8,128)(2,1)}, bf16[128,2,128,128]{3,2,1,0:T(8,128)(2,1)}) custom-call(s32[128]{0:T(128)} %lens.1, bf16[128,4096]{1,0:T(8,128)(2,1)} %hid.3, bf16[1,4096]{1,0:T(2,128)(2,1)} %reshape.12.gain, bf16[4096,1024]{1,0:T(8,128)(2,1)} %wq.1, ...), custom_call_target="tpu_custom_call" | custom-call | tf_op jit(solution)/shard_map/block_attention/pallas_call | solution.py:168
  36.1 65.2 %exchange_mlp.1 = bf16[128,4096]{1,0:T(8,128)(2,1)} custom-call(bf16[128,4096]{1,0:T(8,128)(2,1)} %hid.3, f32[8,128,128]{2,1,0:T(8,128)} %get-tuple-element.7.o_in, f32[2,8,128]{2,1,0:T(8,128)} %get-tuple-element.8.st_in, bf16[1,4096]{1,0:T(2,128)(2,1)} %reshape.13.gain, bf16[1024,4096]{1,0:T(8,128)(2,1)} %wo.1, bf16[4096,3584]{1,0:T(8,128)(2,1)} %wg.1, ...), custom_call_target="tpu_custom_call" | custom-call | tf_op jit(solution)/shard_map/exchange_mlp/pallas_call | solution.py:444
  101.3 2.3 %copy.17 = bf16[128,4096]{1,0:T(8,128)(2,1)} copy(bf16[128,4096]{1,0:T(8,128)(2,1)} %exchange_mlp.1) | data formatting | bytes 2097152

commit v2 on v1

--- a/solution.py
+++ b/solution.py
@@ -13,6 +13,7 @@
 MESH = pl.DeviceIdType.MESH
 CORES = 2
 COLS = 256
+LANES = 128
 VMEM_LIMIT = 66_000_000
 
 
@@ -20,8 +21,8 @@
     return jnp.dot(a, b, preferred_element_type=F32)
 
 
-def attn_kernel(lens, hid, gain, wq, wk, wv, kc, vc, o_out, st_out, k_out, v_out,
-                hbuf, gbuf, ubuf, wbuf, qbuf, knew, vnew, kbuf, vbuf, obuf,
+def attn_kernel(lens_in, hid, gain, wq, wk, wv, kc, vc, o_out, st_out, k_out, v_out,
+                lens, obuf, hbuf, gbuf, ubuf, wbuf, qbuf, knew, vnew, kbuf, vbuf, pbuf,
                 hsem, wsem, kin, vin, kos, vos):
     rows, groups, blk, dim = kc.shape
     heads = wq.shape[1] // dim
@@ -44,59 +45,53 @@
 
     hcopy = pltpu.make_async_copy(hid, hbuf, hsem.at[0])
     gcopy = pltpu.make_async_copy(gain, gbuf, hsem.at[1])
+    lcopy = pltpu.make_async_copy(lens_in, lens, hsem.at[2])
+    lcopy.start()
     hcopy.start()
     gcopy.start()
-    wcopies = []
-    for src, n in ((wq, nq), (wk, nkv), (wv, nkv)):
-        for j in range(n):
-            t = len(wcopies)
-            wcopies.append(pltpu.make_async_copy(src.at[:, pl.ds(j * COLS, COLS)], wbuf.at[t], wsem.at[t]))
-    for cp in wcopies:
-        cp.start()
-    for i in range(2):
+    per = COLS // dim
+
+    def weight(src, j, t):
+        return pltpu.make_async_copy(src.at[:, pl.ds(j * COLS, COLS)], wbuf.at[t], wsem.at[t])
+
+    weights = [weight(wk, j, j) for j in range(nkv)] + [weight(wv, j, nkv + j) for j in range(nkv)]
+    weights += [weight(wq, j, 2 * nkv + j) for j in range(nq)]
+    for cp in weights:
+        cp.start()
+    issued = 1
+    for i in range(issued):
         for cp in load(i):
             cp.start()
+    lcopy.wait()
     hcopy.wait()
     gcopy.wait()
-    g = gbuf[...].astype(F32)
+    g_rows = gbuf[...].astype(F32)
     for r in range(0, rows, 16):
         wide = hbuf[r:r + 16, :].astype(F32)
         inv = lax.rsqrt(jnp.mean(wide * wide, axis=-1, keepdims=True) + NORM_EPS)
-        ubuf[r:r + 16, :] = (wide * inv * g).astype(BF16)
-
-    issued = 2
-    for t, cp in enumerate(wcopies):
+        for j in range(gbuf.shape[0]):
+            sl = slice(j * LANES, (j + 1) * LANES)
+            ubuf[r:r + 16, sl] = (wide[:, sl] * inv * g_rows[j:j + 1, :]).astype(BF16)
+
+    for t, cp in enumerate(weights):
         cp.wait()
         if issued < nchunk:
             for c2 in load(issued):
                 c2.start()
             issued += 1
         res = dot32(ubuf[...], wbuf[t])
-        per = COLS // dim
         for s in range(per):
             part = res[:, s * dim:(s + 1) * dim]
-            if t < nq:
-                qbuf[pl.ds(t * per + s, rows, stride=heads), :] = part
-            elif t < nq + nkv:
-                knew[(t - nq) * per + s] = part
+            if t < nkv:
+                knew[t * per + s] = part
+            elif t < 2 * nkv:
+                vnew[(t - nkv) * per + s] = part
             else:
-                vnew[(t - nq - nkv) * per + s] = part
-    while issued < nchunk:
-        for c2 in load(issued):
-            c2.start()
-        issued += 1
-
-    pair = 2 * heads
-    row_id = lax.broadcasted_iota(jnp.int32, (pair, blk), 0)
-    lane_id = lax.broadcasted_iota(jnp.int32, (pair, blk), 1)
-    first = row_id < heads
-    low = (row_id % heads) < rep
-    stat_lane = lax.broadcasted_iota(jnp.int32, (heads, rows), 1)
+                qbuf[(t - 2 * nkv) * per + s] = part
+
     tile_row = lax.broadcasted_iota(jnp.int32, (16, dim), 0)
-    scale = dim ** -0.5
-
-    def chunk(i, carry):
-        m_acc, l_acc = carry
+
+    def update(i):
         for cp in load(i):
             cp.wait()
 
@@ -115,45 +110,69 @@
                 vbuf[b, gi, pl.ds(t16, 16), :] = jnp.where(mask, jnp.broadcast_to(vnew[gi, pl.ds(b, 1), :], (16, dim)).astype(BF16), vt)
             return 0
 
-        lax.fori_loop(0, crow, patch, 0)
+        lax.fori_loop(0, crow, patch, 0, unroll=4)
         for cp in store(i):
             cp.start()
 
+    ahead = 2
+    for i in range(ahead):
+        update(i)
+
+    slot_id = lax.broadcasted_iota(jnp.int32, (blk, rep * crow), 0)
+    lane_b = lax.broadcasted_iota(jnp.int32, (1, heads * crow), 1) % crow
+    low = lax.broadcasted_iota(jnp.int32, (heads, blk), 0) < rep
+    scale = dim ** -0.5
+    ms, ls = [], []
+
+    for i in range(nchunk):
+        if i + ahead < nchunk:
+            update(i + ahead)
+        b0 = i * crow
+        qt = jnp.concatenate([qbuf[h, b0:b0 + crow, :] for h in range(heads)], axis=0).T
+        limit = jnp.zeros((1, heads * crow), jnp.int32)
+        for r in range(crow):
+            limit = jnp.where(lane_b == r, lens[b0 + r] - base, limit)
+        rhs = [jnp.concatenate([jnp.where(lane_b[:, :rep * crow] == r, qt[:, gi * rep * crow:(gi + 1) * rep * crow], 0.0).astype(BF16) for r in range(crow)], axis=0) for gi in range(groups)]
+        sts = [dot32(jnp.concatenate([kbuf[b0 + r, gi] for r in range(crow)], axis=1), rhs[gi]) for gi in range(groups)]
+        mrow, lrow = [], []
+        for gi in range(groups):
+            lanes = slice(gi * rep * crow, (gi + 1) * rep * crow)
+            s = sts[gi] * scale
+            valid = slot_id <= limit[:, lanes]
+            s = jnp.where(valid, s, MASK_VALUE)
+            m = jnp.max(s, axis=0, keepdims=True)
+            p = jnp.where(valid, jnp.exp(s - m), 0.0)
+            mrow.append(m)
+            lrow.append(jnp.sum(p, axis=0, keepdims=True))
+            pbuf[gi * rep * crow:(gi + 1) * rep * crow, :] = p.T
+        ms.append(mrow)
+        ls.append(lrow)
         for r in range(0, crow, 2):
-            b = i * crow + r
-            q16 = qbuf[pl.ds(pl.multiple_of(b * heads, pair), pair), :]
-            lhs = jnp.concatenate([jnp.where(first, q16, 0.0), jnp.where(first, 0.0, q16)], axis=1).astype(BF16)
-            keys = jnp.concatenate([kbuf[b].reshape(groups * blk, dim), kbuf[b + 1].reshape(groups * blk, dim)], axis=1)
-            sc = lax.dot_general(lhs, keys, (((1,), (1,)), ((), ())), preferred_element_type=F32)
-            s = jnp.where(low, sc[:, :blk], sc[:, blk:]) * scale
-            limit = jnp.where(first, lens[b] - base, lens[b + 1] - base)
-            valid = lane_id <= limit
-            s = jnp.where(valid, s, MASK_VALUE)
-            m = jnp.max(s, axis=1, keepdims=True)
-            p = jnp.where(valid, jnp.exp(s - m), 0.0)
-            tot = jnp.sum(p, axis=1, keepdims=True)
-            pcat = jnp.concatenate([jnp.where(low, p, 0.0), jnp.where(low, 0.0, p)], axis=1).astype(BF16)
-            vals = jnp.concatenate([vbuf[b].reshape(groups * blk, dim), vbuf[b + 1].reshape(groups * blk, dim)], axis=1)
-            mix = dot32(pcat, vals)
-            obuf[pl.ds(pl.multiple_of(b * heads, pair), heads), :] = mix[:heads, :dim]
-            obuf[pl.ds(pl.multiple_of(b * heads + heads, heads), heads), :] = mix[heads:, dim:]
-            m_acc = jnp.where(stat_lane == b, m[:heads], jnp.where(stat_lane == b + 1, m[heads:], m_acc))
-            l_acc = jnp.where(stat_lane == b, tot[:heads], jnp.where(stat_lane == b + 1, tot[heads:], l_acc))
-        return m_acc, l_acc
-
-    zero = jnp.zeros((heads, rows), F32)
-    m_acc, l_acc = lax.fori_loop(0, nchunk, chunk, (zero, zero))
+            lhs = []
+            for q in range(2):
+                ps = pbuf[pl.ds(r + q, heads, stride=crow), :]
+                lhs.append(jnp.concatenate([jnp.where(low, ps, 0.0), jnp.where(low, 0.0, ps)], axis=1))
+            vals = jnp.concatenate([vbuf[b0 + r].reshape(groups * blk, dim), vbuf[b0 + r + 1].reshape(groups * blk, dim)], axis=1)
+            mix = dot32(jnp.concatenate(lhs, axis=0).astype(BF16), vals)
+            obuf[pl.ds(b0 + r, heads, stride=rows), :] = mix[:heads, :dim]
+            obuf[pl.ds(b0 + r + 1, heads, stride=rows), :] = mix[heads:, dim:]
+
+    ocopy = pltpu.make_async_copy(obuf, o_out, hsem.at[3])
+    ocopy.start()
     half = heads // CORES
     for ci in range(CORES):
-        st_out[ci] = jnp.concatenate([m_acc[ci * half:(ci + 1) * half], l_acc[ci * half:(ci + 1) * half]], axis=0)
-    for h in range(heads):
-        o_out[h] = obuf[pl.ds(h, rows, stride=heads), :]
+        for h in range(half):
+            gi, ri = divmod(ci * half + h, rep)
+            lanes = slice(ri * crow, (ri + 1) * crow)
+            st_out[ci, h:h + 1, :] = jnp.concatenate([mrow[gi][:, lanes] for mrow in ms], axis=1)
+            st_out[ci, half + h:half + h + 1, :] = jnp.concatenate([lrow[gi][:, lanes] for lrow in ls], axis=1)
 
     def drain(i, _):
         for cp in store(i):
             cp.wait()
         return 0
 
+    ocopy.wait()
     lax.fori_loop(0, nchunk, drain, 0)
 
 
@@ -162,30 +181,32 @@
     heads = w_q.shape[1] // dim
     width = w_q.shape[0]
     nw = (w_q.shape[1] + w_k.shape[1] + w_v.shape[1]) // COLS
-    nchunk = 8
+    nchunk = 4
     any_spec = pl.BlockSpec(memory_space=pl.ANY)
     vm = pl.BlockSpec(memory_space=pltpu.VMEM)
     return pl.pallas_call(
         attn_kernel,
         name='block_attention',
-        out_shape=(jax.ShapeDtypeStruct((heads, rows, dim), F32),
+        out_shape=(jax.ShapeDtypeStruct((heads * rows, dim), F32),
                    jax.ShapeDtypeStruct((CORES, heads, rows), F32),
                    jax.ShapeDtypeStruct(k_cache.shape, BF16),
                    jax.ShapeDtypeStruct(v_cache.shape, BF16)),
-        in_specs=[pl.BlockSpec(memory_space=pltpu.SMEM)] + [any_spec] * 7,
-        out_specs=(vm, vm, any_spec, any_spec),
+        in_specs=[any_spec] * 8,
+        out_specs=(any_spec, vm, any_spec, any_spec),
         scratch_shapes=[
+            pltpu.SMEM((rows,), jnp.int32),
+            pltpu.VMEM((heads * rows, dim), F32),
             pltpu.VMEM((rows, width), BF16),
-            pltpu.VMEM((1, width), BF16),
+            pltpu.VMEM((width // LANES, LANES), BF16),
             pltpu.VMEM((rows, width), BF16),
             pltpu.VMEM((nw, width, COLS), BF16),
-            pltpu.VMEM((rows * heads, dim), F32),
+            pltpu.VMEM((heads, rows, dim), F32),
             pltpu.VMEM((groups, rows, dim), F32),
             pltpu.VMEM((groups, rows, dim), F32),
             pltpu.VMEM(k_cache.shape, BF16),
             pltpu.VMEM(v_cache.shape, BF16),
-            pltpu.VMEM((rows * heads, dim), F32),
-            pltpu.SemaphoreType.DMA((2,)),
+            pltpu.VMEM((heads * rows // nchunk, blk), F32),
+            pltpu.SemaphoreType.DMA((4,)),
             pltpu.SemaphoreType.DMA((nw,)),
             pltpu.SemaphoreType.DMA((nchunk,)),
             pltpu.SemaphoreType.DMA((nchunk,)),
@@ -193,13 +214,13 @@
             pltpu.SemaphoreType.DMA((nchunk,)),
         ],
         compiler_params=pltpu.CompilerParams(vmem_limit_bytes=VMEM_LIMIT),
-    )(seq_lens, hidden, gain.reshape(1, width), w_q, w_k, w_v, k_cache, v_cache)
+    )(seq_lens, hidden, gain.reshape(width // LANES, LANES), w_q, w_k, w_v, k_cache, v_cache)
 
 
 def mlp_kernel(nx, ny, hid, o_in, st_in, gain, wo, wg, wu, wd, out,
                wo_b, wg_b, wu_b, wd_b, hid_b, gain_b, o_b, st_b, po_b, pst_b, oc_b, cst_b, xo_b, xst_b, tst_b,
                att_b, pw_b, rw_b, mid_b, u2_b, act_b, ab_b, pd_b, rd_b, fin_b,
-               lsem, wsem, ds_s, ds_r, xs_s, xs_r, as_s, as_r, ws_s, ws_r, ms_s, ms_r, cs_s, cs_r, dn_s, dn_r, fs_s, fs_r, fp_s, fp_r):
+               lsem, osem, gsem, usem, dsem, ds_s, ds_r, xs_s, xs_r, as_s, as_r, ws_s, ws_r, ms_s, ms_r, cs_s, cs_r, dn_s, dn_r, fs_s, fs_r, fp_s, fp_r):
     sp = lax.axis_index('sp')
     y = lax.axis_index('tp')
     x = sp // CORES
@@ -207,7 +228,7 @@
     oc = 1 - c
     half_h, rows, dim = po_b.shape
     xr = rows // nx
-    width = gain.shape[1]
+    width = gain.shape[0] * LANES
     hw = width // CORES
     cw = hw // ny
     partner = {'tp': y, 'sp': x * CORES + oc}
@@ -229,15 +250,26 @@
     ]
     for cp in loads:
         cp.start()
-    inner = wg_b.shape[1]
-    w_loads = [
-        pltpu.make_async_copy(wo.at[:, cols(c, hw)], wo_b, wsem.at[0]),
-        pltpu.make_async_copy(wg.at[:, cols(c, inner)], wg_b, wsem.at[1]),
-        pltpu.make_async_copy(wu.at[:, cols(c, inner)], wu_b, wsem.at[2]),
-        pltpu.make_async_copy(wd.at[:, cols(c, hw)], wd_b, wsem.at[3]),
-    ]
-    for cp in w_loads:
-        cp.start()
+    steps = wg_b.shape[0]
+    inner = steps * COLS
+    def row_load(w, w_b, sem, n, j):
+        r = cols(j, w_b.shape[0] // n)
+        return pltpu.make_async_copy(w.at[r, cols(c, hw)], w_b.at[r], sem.at[j])
+
+    def col_loads(j):
+        r = cols(c * steps + j, COLS)
+        return (pltpu.make_async_copy(wg.at[:, r], wg_b.at[j], gsem.at[j]), pltpu.make_async_copy(wu.at[:, r], wu_b.at[j], usem.at[j]))
+
+    wo_loads = [row_load(wo, wo_b, osem, osem.shape[0], j) for j in range(osem.shape[0])]
+    wd_loads = [row_load(wd, wd_b, dsem, steps, j) for j in range(steps)]
+    for cp in wo_loads:
+        cp.start(priority=1)
+    for cp in col_loads(0):
+        cp.start(priority=1)
+    for cp in col_loads(1):
+        cp.start(priority=1)
+    for cp in col_loads(2):
+        cp.start(priority=1)
 
     barrier = pltpu.get_barrier_semaphore()
     pl.semaphore_signal(barrier, inc=1, device_id=partner, device_id_type=MESH)
@@ -272,6 +304,10 @@
         sends.append(rcopy(oc_b.at[:, pl.ds(xx * xr, xr), :], xo_b.at[x], xs_s.at[k - 1, 1], xs_r.at[x, 1], peer(y, xx)))
     for cp in sends:
         cp.start()
+    for cp in col_loads(3):
+        cp.start(priority=1)
+    for cp in col_loads(4):
+        cp.start(priority=1)
     tst_b[0] = cst_b[...].T
     for k in range(1, nx):
         xx = (x + k) % nx
@@ -319,7 +355,8 @@
             cp.wait_send()
         return total
 
-    w_loads[0].wait()
+    for cp in wo_loads:
+        cp.wait()
     total = reduce_y(lambda: jnp.concatenate([att_b[0], att_b[1]], axis=1).astype(BF16), wo_b, pw_b, rw_b, ws_s, ws_r)
     mid_b[c, y] = (hid_b[...].astype(F32) + total).astype(BF16).astype(F32)
 
@@ -329,6 +366,10 @@
         started.append(rcopy(mid_b.at[c, y], mid_b.at[c, y], ms_s.at[k], ms_r.at[y], peer(yy, x)))
     for cp in started:
         cp.start()
+    for cp in col_loads(5):
+        cp.start(priority=1)
+    for cp in col_loads(6):
+        cp.start(priority=1)
     for k in range(1, ny):
         yy = (y + k) % ny
         rcopy(mid_b.at[c, yy], mid_b.at[c, yy], ms_s.at[k], ms_r.at[yy], peer(yy, x)).wait_recv()
@@ -344,25 +385,34 @@
             v = mid_b[ci, yi]
             sq = sq + jnp.sum(v * v, axis=-1, keepdims=True)
     inv = lax.rsqrt(sq / width + NORM_EPS)
+    g_rows = gain_b[...].astype(F32)
     for ci in range(CORES):
         for yi in range(ny):
             o = ci * hw + yi * cw
-            u2_b[:, o:o + cw] = (mid_b[ci, yi] * inv * gain_b[:, o:o + cw].astype(F32)).astype(BF16)
+            for j in range(cw // LANES):
+                row = o // LANES + j
+                u2_b[:, o + j * LANES:o + (j + 1) * LANES] = (mid_b[ci, yi, :, j * LANES:(j + 1) * LANES] * inv * g_rows[row:row + 1, :]).astype(BF16)
     for cp in started:
         cp.wait_send()
 
-    w_loads[1].wait()
-    w_loads[2].wait()
-    steps = inner // COLS
 
     def gate_up(j, _):
+        for cp in col_loads(j):
+            cp.wait()
         lhs = u2_b[...]
-        gp = dot32(lhs, wg_b[:, cols(j, COLS)])
-        up = dot32(lhs, wu_b[:, cols(j, COLS)])
+        gp = dot32(lhs, wg_b[j])
+        up = dot32(lhs, wu_b[j])
         act_b[c, j] = (gp * jax.nn.sigmoid(gp) * up).astype(BF16).astype(F32)
         rcopy(act_b.at[c, j], act_b.at[c, j], dn_s.at[j], dn_r.at[j], partner).start()
         return 0
 
+    wd_loads[0].start(priority=1)
+    wd_loads[1].start(priority=1)
+    wd_loads[2].start(priority=1)
+    wd_loads[3].start(priority=1)
+    wd_loads[4].start(priority=1)
+    wd_loads[5].start(priority=1)
+    wd_loads[6].start(priority=1)
     lax.fori_loop(0, steps, gate_up, 0)
 
     def take(j, _):
@@ -372,7 +422,8 @@
         return 0
 
     lax.fori_loop(0, steps, take, 0)
-    w_loads[3].wait()
+    for cp in wd_loads:
+        cp.wait()
     total = reduce_y(lambda: ab_b[...], wd_b, pd_b, rd_b, fs_s, fs_r)
     fin_b[x, y, c] = (mid_b[c, y] + total).astype(BF16).astype(F32)
 
@@ -449,11 +500,11 @@
         out_specs=pl.BlockSpec(memory_space=pltpu.VMEM),
         scratch_shapes=[
             pltpu.VMEM((w_o.shape[0], hw), BF16),
-            pltpu.VMEM((width, inner), BF16),
-            pltpu.VMEM((width, inner), BF16),
+            pltpu.VMEM((steps, width, COLS), BF16),
+            pltpu.VMEM((steps, width, COLS), BF16),
             pltpu.VMEM((w_down.shape[0], hw), BF16),
             pltpu.VMEM((xr, cw), BF16),
-            pltpu.VMEM((1, width), BF16),
+            pltpu.VMEM((width // LANES, LANES), BF16),
             pltpu.VMEM((heads, rows, dim), F32),
             pltpu.VMEM((CORES, heads, rows), F32),
             pltpu.VMEM((half_h, rows, dim), F32),
@@ -473,7 +524,7 @@
             pltpu.VMEM((ny, xr, cw), F32),
             pltpu.VMEM((ny, xr, cw), F32),
             pltpu.VMEM((nx, ny, CORES, xr, cw), F32),
-            dma((4,)), dma((4,)),
+            dma((4,)), dma((4,)), dma((steps,)), dma((steps,)), dma((steps,)),
             dma((2,)), dma((2,)),
             dma((nx, 2)), dma((nx, 2)),
             dma((1,)), dma((1,)),
@@ -485,7 +536,7 @@
             dma((ny, 2 * nx + ny)), dma((nx, ny, CORES)),
         ],
         compiler_params=pltpu.CompilerParams(vmem_limit_bytes=VMEM_LIMIT, collective_id=0, has_side_effects=True),
-    )(hidden, o_part, stats, gain.reshape(1, width), w_o, w_gate, w_up, w_down)
+    )(hidden, o_part, stats, gain.reshape(width // LANES, LANES), w_o, w_gate, w_up, w_down)
 
 
 def solution(mesh):
@@ -497,6 +548,7 @@
 
     def local_step(hidden, seq_lens, k_cache, v_cache, attn_norm, w_q, w_k, w_v, w_o, mlp_norm, w_gate, w_up, w_down):
         o_part, stats, k_out, v_out = attention(hidden, seq_lens, k_cache, v_cache, attn_norm, w_q, w_k, w_v)
+        o_part = o_part.reshape(stats.shape[1], stats.shape[2], k_cache.shape[3])
         hidden_out = mlp(mesh, hidden, o_part, stats, mlp_norm, w_o, w_gate, w_up, w_down)
         return hidden_out, k_out, v_out
 

time: 104 us -> 77.2 us (0.74)
  Pallas kernels: 98.1 us -> 74.1 us
  local copies, waits for them, and re-layouts: 4.9 us -> 2.29 us
    pallas_call x1, Pallas kernels: 32.9 us -> 17.3 us  [attention(): pl.pallas_call(attn_kernel, name='block_attention', out_shape=(jax.ShapeD...]
    pallas_call x1, Pallas kernels: 65.2 us -> 56.8 us  [mlp(): pl.pallas_call(functools.partial(mlp_kernel, nx, ny), name='exchange_mlp'...]
    reshape x2 -> x0, local copies, waits for them, and re-layouts: 2.61 us -> none  [the longest x1 1.31 us: attention(): gain.reshape(1, width)]
where the time goes in v2:
time: 77.2 us; the launch traced here: 77.1 us
  Pallas kernels  74.1 us (96%)
  local copies, waits for them, and re-layouts  2.29 us (3%)
    pallas_call x1, Pallas kernels, mlp(): pl.pallas_call(functools.partial(mlp_kernel, nx, ny), name='exchange_mlp'...  56.8 us
    pallas_call x1, Pallas kernels, attention(): pl.pallas_call(attn_kernel, name='block_attention', out_shape=(jax.ShapeD...  17.3 us
    unnamed x1, local copies, waits for them, and re-layouts  2.29 us

profile of v2, /device:TPU:97, one launch (start us, length us, event | category | flops | bytes accessed | tf_op | source)
XLA Modules:
  0.0 77.1 jit_solution(2436511281083822079)
XLA Ops:
  0.6 17.3 %block_attention.1 = (f32[1024,128]{1,0:T(8,128)}, f32[2,8,128]{2,1,0:T(8,128)}, bf16[128,2,128,128]{3,2,1,0:T(8,128)(2,1)}, bf16[128,2,128,128]{3,2,1,0:T(8,128)(2,1)}) custom-call(s32[128]{0:T(128)} %lens_in.1, bf16[128,4096]{1,0:T(8,128)(2,1)} %hid.3, bf16[32,128]{1,0:T(8,128)(2,1)} %bitcast.4, bf16[4096,1024]{1,0:T(8,128)(2,1)} %wq.1, ...), custom_call_target="tpu_custom_call" | custom-call | tf_op jit(solution)/shard_map/block_attention/pallas_call | solution.py:187
  17.9 56.8 %exchange_mlp.1 = bf16[128,4096]{1,0:T(8,128)(2,1)} custom-call(bf16[128,4096]{1,0:T(8,128)(2,1)} %hid.3, f32[8,128,128]{2,1,0:T(8,128)} %bitcast.3, f32[2,8,128]{2,1,0:T(8,128)} %get-tuple-element.8.st_in, bf16[32,128]{1,0:T(8,128)(2,1)} %bitcast.5, bf16[1024,4096]{1,0:T(8,128)(2,1)} %wo.1, bf16[4096,3584]{1,0:T(8,128)(2,1)} %wg.1, bf16[4096,3584]{1,0:T(8,128)(2,1)} %wu.1, ...), custom_call_target="tpu_custom_call" | custom-call | tf_op jit(solution)/shard_map/exchange_mlp/pallas_call | solution.py:495
  74.8 2.3 %copy.17 = bf16[128,4096]{1,0:T(8,128)(2,1)} copy(bf16[128,4096]{1,0:T(8,128)(2,1)} %exchange_mlp.1) | data formatting | bytes 2097152

commit v3 on v2

--- a/solution.py
+++ b/solution.py
@@ -14,7 +14,8 @@
 CORES = 2
 COLS = 256
 LANES = 128
-VMEM_LIMIT = 66_000_000
+QCOLS = 256
+VMEM_LIMIT = 60_000_000
 
 
 def dot32(a, b):
@@ -218,9 +219,10 @@
 
 
 def mlp_kernel(nx, ny, hid, o_in, st_in, gain, wo, wg, wu, wd, out,
-               wo_b, wg_b, wu_b, wd_b, hid_b, gain_b, o_b, st_b, po_b, pst_b, oc_b, cst_b, xo_b, xst_b, tst_b,
-               att_b, pw_b, rw_b, mid_b, u2_b, act_b, ab_b, pd_b, rd_b, fin_b,
-               lsem, osem, gsem, usem, dsem, ds_s, ds_r, xs_s, xs_r, as_s, as_r, ws_s, ws_r, ms_s, ms_r, cs_s, cs_r, dn_s, dn_r, fs_s, fs_r, fp_s, fp_r):
+               wo_b, wg_b, wu_b, wd_b, hid_b, gain_b, gf_b, o_b, st_b, po_b, pst_b, oc_b, cst_b, xo_b, xst_b, tst_b,
+               att_b, pw_b, rw_b, mid_b, ss_b, g_acc, u_acc, act_b, ab_b, pd_b, rd_b, fin_b,
+               lsem, osem, gsem, usem, dsem, ds_s, ds_r, xs_s, xs_r, as_s, as_r, ws_s, ws_r, ms_s, ms_r, cs_s, ss_s, ss_r,
+               dn_s, dn_r, fs_s, fs_r, fp_s, fp_r):
     sp = lax.axis_index('sp')
     y = lax.axis_index('tp')
     x = sp // CORES
@@ -231,10 +233,16 @@
     width = gain.shape[0] * LANES
     hw = width // CORES
     cw = hw // ny
+    nq, qw = mid_b.shape[2], mid_b.shape[4]
     partner = {'tp': y, 'sp': x * CORES + oc}
+    far = [2, 1, 3] if ny == 4 else list(range(1, ny))
+    near = [1, 3, 2] if ny == 4 else list(range(1, ny))
 
     def peer(yy, xx):
         return {'tp': yy, 'sp': xx * CORES + c}
+
+    def cross(yy):
+        return {'tp': yy, 'sp': x * CORES + oc}
 
     def rcopy(src, dst, ssem, rsem, dev):
         return pltpu.make_async_remote_copy(src_ref=src, dst_ref=dst, send_sem=ssem, recv_sem=rsem, device_id=dev, device_id_type=MESH)
@@ -252,6 +260,7 @@
         cp.start()
     steps = wg_b.shape[0]
     inner = steps * COLS
+
     def row_load(w, w_b, sem, n, j):
         r = cols(j, w_b.shape[0] // n)
         return pltpu.make_async_copy(w.at[r, cols(c, hw)], w_b.at[r], sem.at[j])
@@ -262,14 +271,21 @@
 
     wo_loads = [row_load(wo, wo_b, osem, osem.shape[0], j) for j in range(osem.shape[0])]
     wd_loads = [row_load(wd, wd_b, dsem, steps, j) for j in range(steps)]
+    gu_plan = [range(0, 3), range(3, 5), range(5, steps)]
+    wd_plan = [range(0, 4), range(4, steps)]
+
+    def fetch_gu(stage):
+        for j in gu_plan[stage]:
+            for cp in col_loads(j):
+                cp.start(priority=1)
+
+    def fetch_wd(stage):
+        for j in wd_plan[stage]:
+            wd_loads[j].start(priority=1)
+
     for cp in wo_loads:
         cp.start(priority=1)
-    for cp in col_loads(0):
-        cp.start(priority=1)
-    for cp in col_loads(1):
-        cp.start(priority=1)
-    for cp in col_loads(2):
-        cp.start(priority=1)
+    fetch_gu(0)
 
     barrier = pltpu.get_barrier_semaphore()
     pl.semaphore_signal(barrier, inc=1, device_id=partner, device_id_type=MESH)
@@ -277,14 +293,17 @@
         pl.semaphore_signal(barrier, inc=1, device_id=peer(y, (x + k) % nx), device_id_type=MESH)
     for k in range(1, ny):
         pl.semaphore_signal(barrier, inc=1, device_id=peer((y + k) % ny, x), device_id_type=MESH)
+        pl.semaphore_signal(barrier, inc=1, device_id=cross((y + k) % ny), device_id_type=MESH)
     for cp in loads:
         cp.wait()
-    pl.semaphore_wait(barrier, 1 + (nx - 1) + (ny - 1))
+    gf_b[...] = gain_b[...].astype(F32)
+    pl.semaphore_wait(barrier, 1 + (nx - 1) + 2 * (ny - 1))
 
     d2d = [rcopy(o_b.at[pl.ds(half_h * oc, half_h)], po_b, ds_s.at[0], ds_r.at[0], partner),
            rcopy(st_b.at[oc], pst_b, ds_s.at[1], ds_r.at[1], partner)]
     for cp in d2d:
         cp.start()
+    fetch_gu(1)
     for cp in d2d:
         cp.wait()
     s0 = st_b[c]
@@ -304,10 +323,7 @@
         sends.append(rcopy(oc_b.at[:, pl.ds(xx * xr, xr), :], xo_b.at[x], xs_s.at[k - 1, 1], xs_r.at[x, 1], peer(y, xx)))
     for cp in sends:
         cp.start()
-    for cp in col_loads(3):
-        cp.start(priority=1)
-    for cp in col_loads(4):
-        cp.start(priority=1)
+    fetch_gu(2)
     tst_b[0] = cst_b[...].T
     for k in range(1, nx):
         xx = (x + k) % nx
@@ -336,146 +352,208 @@
     rcopy(att_b.at[oc], att_b.at[oc], as_s.at[0], as_r.at[0], partner).wait_recv()
     swap.wait_send()
 
-    def reduce_y(lhs_of, w_b, send_b, recv_b, s_sem, r_sem):
-        lhs = lhs_of()
-        started = []
-        for k in [2, 1, 3, 0] if ny == 4 else list(range(1, ny)) + [0]:
+    def unit(yy, q):
+        return pl.ds(pl.multiple_of(yy * cw + q * qw, qw), qw)
+
+    def send_unit(send_b, recv_b, s_sem, r_sem, q, k):
+        yy = (y + k) % ny
+        cp = rcopy(send_b.at[q, yy], recv_b.at[q, y], s_sem.at[q, k], r_sem.at[q, y], peer(yy, x))
+        cp.start()
+        return cp
+
+    def collect(send_b, recv_b, s_sem, r_sem, q):
+        total = send_b[q, y]
+        for k in range(1, ny):
             yy = (y + k) % ny
-            send_b[yy] = dot32(lhs, w_b[:, cols(yy, cw)])
+            rcopy(send_b.at[q, yy], recv_b.at[q, yy], s_sem.at[q, k], r_sem.at[q, yy], peer(yy, x)).wait_recv()
+            total = total + recv_b[q, yy]
+        return total
+
+    for cp in wo_loads:
+        cp.wait()
+    lhs = jnp.concatenate([att_b[0], att_b[1]], axis=1).astype(BF16)
+    started = []
+    for q in range(nq):
+        for k in far + [0]:
+            yy = (y + k) % ny
+            pw_b[q, yy] = dot32(lhs, wo_b[:, unit(yy, q)])
             if k:
-                cp = rcopy(send_b.at[yy], recv_b.at[y], s_sem.at[k], r_sem.at[y], peer(yy, x))
+                started.append(send_unit(pw_b, rw_b, ws_s, ws_r, q, k))
+    fetch_wd(0)
+
+    def mid_copy(ci, yy, q, ssem, dev):
+        return rcopy(mid_b.at[ci, yy, q], mid_b.at[ci, yy, q], ssem, ms_r.at[ci, yy, q], dev)
+
+    sq = jnp.zeros((xr, 1), F32)
+    for q in range(nq):
+        piece = (hid_b[:, q * qw:(q + 1) * qw].astype(F32) + collect(pw_b, rw_b, ws_s, ws_r, q)).astype(BF16).astype(F32)
+        mid_b[c, y, q] = piece
+        sq = sq + jnp.sum(piece * piece, axis=-1, keepdims=True)
+        sends = []
+        if q == nq - 1:
+            wide = jnp.broadcast_to(sq, (xr, LANES))
+            ss_b[c, y] = jnp.concatenate([wide] * (LANES // xr), axis=0).T[:ss_b.shape[2]]
+            sends.append(rcopy(ss_b.at[c, y], ss_b.at[c, y], ss_s.at[0, 0], ss_r.at[c, y], partner))
+            for k in range(1, ny):
+                yy = (y + k) % ny
+                sends.append(rcopy(ss_b.at[c, y], ss_b.at[c, y], ss_s.at[0, k], ss_r.at[c, y], peer(yy, x)))
+                sends.append(rcopy(ss_b.at[c, y], ss_b.at[c, y], ss_s.at[1, k], ss_r.at[c, y], cross(yy)))
+        sends.append(mid_copy(c, y, q, cs_s.at[q, 0], partner))
+        for k in far:
+            sends.append(mid_copy(c, y, q, ms_s.at[q, k], peer((y + k) % ny, x)))
+        for cp in sends:
+            cp.start()
+        started += sends
+    fetch_wd(1)
+
+    def ss_wait(ci, yy):
+        rcopy(ss_b.at[ci, yy], ss_b.at[ci, yy], ss_s.at[0, 0], ss_r.at[ci, yy], partner).wait_recv()
+
+    ss_wait(oc, y)
+    for k in range(1, ny):
+        ss_wait(c, (y + k) % ny)
+        ss_wait(oc, (y + k) % ny)
+    tot = ss_b[0, 0]
+    for t in range(1, CORES * ny):
+        tot = tot + ss_b[t // ny, t % ny]
+    inv = lax.rsqrt(tot.T[:xr, :1] / width + NORM_EPS)
+    inv = jnp.broadcast_to(inv, (xr, LANES))
+
+    for j in range(steps):
+        for cp in col_loads(j):
+            cp.wait()
+
+    def accumulate(ci, yy, first):
+        start = ci * hw + yy * cw
+        parts = []
+        for q in range(nq):
+            for j in range(qw // LANES):
+                g = gf_b[pl.ds(start // LANES + q * (qw // LANES) + j, 1), :]
+                parts.append((mid_b[ci, yy, q, :, j * LANES:(j + 1) * LANES] * inv * g).astype(BF16))
+        u = jnp.concatenate(parts, axis=1)
+        r = pl.ds(pl.multiple_of(start, cw), cw)
+        for j in range(steps):
+            gp = dot32(u, wg_b[j, r, :])
+            up = dot32(u, wu_b[j, r, :])
+            g_acc[j] = gp if first else g_acc[j] + gp
+            u_acc[j] = up if first else u_acc[j] + up
+
+    def other(yy):
+        for q in range(nq):
+            mid_copy(oc, yy, q, cs_s.at[q, 0], partner).wait_recv()
+
+    accumulate(c, y, True)
+    other(y)
+    accumulate(oc, y, False)
+
+    def gather_step(i, _):
+        k = i + (i // 2) * (1 - 2 * (i % 2)) if ny == 4 else i
+        yy = (y + k) % ny
+        for q in range(nq):
+            mid_copy(c, yy, q, ms_s.at[q, 0], partner).wait_recv()
+            mid_copy(c, yy, q, cs_s.at[q, k], partner).start()
+        accumulate(c, yy, False)
+        other(yy)
+        accumulate(oc, yy, False)
+        return 0
+
+    lax.fori_loop(1, ny, gather_step, 0)
+    for k in range(1, ny):
+        for q in range(nq):
+            mid_copy(c, (y + k) % ny, q, cs_s.at[q, k], partner).wait_send()
+
+    acts = []
+    for j in range(steps):
+        gp = g_acc[j]
+        act = (gp * jax.nn.sigmoid(gp) * u_acc[j]).astype(BF16)
+        ab_b[c, :, j * COLS:(j + 1) * COLS] = act
+        act_b[c, j] = act.astype(F32)
+        cp = rcopy(act_b.at[c, j], act_b.at[c, j], dn_s.at[j], dn_r.at[j], partner)
+        cp.start()
+        acts.append(cp)
+    for cp in started:
+        cp.wait_send()
+
+    for cp in wd_loads:
+        cp.wait()
+
+    def down(ci, yy, q):
+        return dot32(ab_b[ci], wd_b[cols(ci, inner), unit(yy, q)])
+
+    started = []
+    for k in far + [0]:
+        yy = (y + k) % ny
+        pd_b[0, yy] = down(c, yy, 0)
+    for j in range(steps):
+        rcopy(act_b.at[oc, j], act_b.at[oc, j], dn_s.at[j], dn_r.at[j], partner).wait_recv()
+        ab_b[oc, :, j * COLS:(j + 1) * COLS] = act_b[oc, j].astype(BF16)
+    for q in range(nq):
+        for k in far + [0]:
+            yy = (y + k) % ny
+            rest = down(oc, yy, q)
+            pd_b[q, yy] = (pd_b[q, yy] if q == 0 else down(c, yy, q)) + rest
+            if k:
+                started.append(send_unit(pd_b, rd_b, fs_s, fs_r, q, k))
+
+    def slot(yy, xx, q):
+        return fin_b.at[xx, yy, c, q]
+
+    def place(k1, k2, ci):
+        oi = 1 - ci
+        return (y + k1 * oi + k2 * ci) % ny, (x + k1 * ci + k2 * oi) % nx
+
+    def fcopy(yy, xx, q, ssem, dev):
+        return rcopy(slot(yy, xx, q), slot(yy, xx, q), ssem, fp_r.at[xx, yy, c, q], dev)
+
+    def spread(k1, q):
+        sy, sx = place(k1, 0, c)
+        for k2 in far:
+            ty, tx = place(0, k2, c)
+            cp = fcopy(sy, sx, q, fp_s.at[q, k1, k2], peer(ty, tx))
+            cp.start()
+            started.append(cp)
+        cp = fcopy(sy, sx, q, fp_s.at[q, k1, 0], partner)
+        cp.start()
+        started.append(cp)
+
+    def landed(yy, xx, ci, q):
+        rcopy(fin_b.at[xx, yy, ci, q], fin_b.at[xx, yy, ci, q], fp_s.at[0, 0, 0], fp_r.at[xx, yy, ci, q], partner).wait_recv()
+
+    def emit(yy, xx, ci, q):
+        r = pl.ds(pl.multiple_of(xx * xr, xr), xr)
+        out[r, pl.ds(pl.multiple_of(ci * hw + yy * cw + q * qw, qw), qw)] = fin_b[xx, yy, ci, q].astype(BF16)
+
+    for q in range(nq):
+        fin_b[x, y, c, q] = (mid_b[c, y, q] + collect(pd_b, rd_b, fs_s, fs_r, q)).astype(BF16).astype(F32)
+        for k1 in far:
+            ty, tx = place(k1, 0, c)
+            cp = fcopy(y, x, q, fp_s.at[q, 0, nx + k1], peer(ty, tx))
+            cp.start()
+            started.append(cp)
+        spread(0, q)
+    for q in range(nq):
+        for k1 in near:
+            sy, sx = place(k1, 0, c)
+            landed(sy, sx, c, q)
+            spread(k1, q)
+        emit(y, x, c, q)
+        for k1 in near:
+            emit(*place(k1, 0, c), c, q)
+    for q in range(nq):
+        for k1 in [0] + near:
+            for k2 in near:
+                sy, sx = place(k1, k2, c)
+                landed(sy, sx, c, q)
+                cp = fcopy(sy, sx, q, fp_s.at[q, k1, nx + ny + k2], partner)
                 cp.start()
                 started.append(cp)
-        total = send_b[y]
-        for k in range(1, ny):
-            yy = (y + k) % ny
-            rcopy(send_b.at[yy], recv_b.at[yy], s_sem.at[k], r_sem.at[yy], peer(yy, x)).wait_recv()
-            total = total + recv_b[yy]
-        for cp in started:
-            cp.wait_send()
-        return total
-
-    for cp in wo_loads:
-        cp.wait()
-    total = reduce_y(lambda: jnp.concatenate([att_b[0], att_b[1]], axis=1).astype(BF16), wo_b, pw_b, rw_b, ws_s, ws_r)
-    mid_b[c, y] = (hid_b[...].astype(F32) + total).astype(BF16).astype(F32)
-
-    started = [rcopy(mid_b.at[c, y], mid_b.at[c, y], cs_s.at[0], cs_r.at[y], partner)]
-    for k in range(1, ny):
-        yy = (y + k) % ny
-        started.append(rcopy(mid_b.at[c, y], mid_b.at[c, y], ms_s.at[k], ms_r.at[y], peer(yy, x)))
-    for cp in started:
-        cp.start()
-    for cp in col_loads(5):
-        cp.start(priority=1)
-    for cp in col_loads(6):
-        cp.start(priority=1)
-    for k in range(1, ny):
-        yy = (y + k) % ny
-        rcopy(mid_b.at[c, yy], mid_b.at[c, yy], ms_s.at[k], ms_r.at[yy], peer(yy, x)).wait_recv()
-        cp = rcopy(mid_b.at[c, yy], mid_b.at[c, yy], cs_s.at[k], cs_r.at[yy], partner)
-        cp.start()
-        started.append(cp)
-    for k in range(ny):
-        yy = (y + k) % ny
-        rcopy(mid_b.at[oc, yy], mid_b.at[oc, yy], cs_s.at[k], cs_r.at[yy], partner).wait_recv()
-    sq = jnp.zeros((xr, 1), F32)
-    for ci in range(CORES):
-        for yi in range(ny):
-            v = mid_b[ci, yi]
-            sq = sq + jnp.sum(v * v, axis=-1, keepdims=True)
-    inv = lax.rsqrt(sq / width + NORM_EPS)
-    g_rows = gain_b[...].astype(F32)
-    for ci in range(CORES):
-        for yi in range(ny):
-            o = ci * hw + yi * cw
-            for j in range(cw // LANES):
-                row = o // LANES + j
-                u2_b[:, o + j * LANES:o + (j + 1) * LANES] = (mid_b[ci, yi, :, j * LANES:(j + 1) * LANES] * inv * g_rows[row:row + 1, :]).astype(BF16)
-    for cp in started:
-        cp.wait_send()
-
-
-    def gate_up(j, _):
-        for cp in col_loads(j):
-            cp.wait()
-        lhs = u2_b[...]
-        gp = dot32(lhs, wg_b[j])
-        up = dot32(lhs, wu_b[j])
-        act_b[c, j] = (gp * jax.nn.sigmoid(gp) * up).astype(BF16).astype(F32)
-        rcopy(act_b.at[c, j], act_b.at[c, j], dn_s.at[j], dn_r.at[j], partner).start()
-        return 0
-
-    wd_loads[0].start(priority=1)
-    wd_loads[1].start(priority=1)
-    wd_loads[2].start(priority=1)
-    wd_loads[3].start(priority=1)
-    wd_loads[4].start(priority=1)
-    wd_loads[5].start(priority=1)
-    wd_loads[6].start(priority=1)
-    lax.fori_loop(0, steps, gate_up, 0)
-
-    def take(j, _):
-        rcopy(act_b.at[oc, j], act_b.at[oc, j], dn_s.at[j], dn_r.at[j], partner).wait()
-        for ci in range(CORES):
-            ab_b[:, pl.ds(pl.multiple_of(ci * inner + j * COLS, COLS), COLS)] = act_b[ci, j].astype(BF16)
-        return 0
-
-    lax.fori_loop(0, steps, take, 0)
-    for cp in wd_loads:
-        cp.wait()
-    total = reduce_y(lambda: ab_b[...], wd_b, pd_b, rd_b, fs_s, fs_r)
-    fin_b[x, y, c] = (mid_b[c, y] + total).astype(BF16).astype(F32)
-
-    def slot(yy, xx):
-        return fin_b.at[xx, yy, c]
-
-    def place(k1, k2):
-        return (y + k1 * oc + k2 * c) % ny, (x + k1 * c + k2 * oc) % nx
-
-    started = []
-
-    def spread(k1):
-        sy, sx = place(k1, 0)
-        for k2 in [2, 1, 3] if nx == 4 else range(1, nx):
-            ty, tx = place(0, k2)
-            cp = rcopy(slot(sy, sx), slot(sy, sx), fp_s.at[k1, k2], fp_r.at[sx, sy, c], peer(ty, tx))
-            cp.start()
-            started.append(cp)
-        cp = rcopy(slot(sy, sx), slot(sy, sx), fp_s.at[k1, 0], fp_r.at[sx, sy, c], partner)
-        cp.start()
-        started.append(cp)
-
-    for k1 in [2, 1, 3] if ny == 4 else range(1, ny):
-        ty, tx = place(k1, 0)
-        cp = rcopy(slot(y, x), slot(y, x), fp_s.at[0, nx + k1], fp_r.at[x, y, c], peer(ty, tx))
-        cp.start()
-        started.append(cp)
-    spread(0)
-
-    def arrived(yy, xx, ci):
-        return rcopy(fin_b.at[xx, yy, ci], fin_b.at[xx, yy, ci], fp_s.at[0, 0], fp_r.at[xx, yy, ci], partner)
-
-    for k1 in [1, 3, 2] if ny == 4 else range(1, ny):
-        sy, sx = place(k1, 0)
-        arrived(sy, sx, c).wait_recv()
-        spread(k1)
-    for k1 in [0, 1, 3, 2] if ny == 4 else range(ny):
-        for k2 in [1, 3, 2] if nx == 4 else range(1, nx):
-            sy, sx = place(k1, k2)
-            arrived(sy, sx, c).wait_recv()
-            cp = rcopy(slot(sy, sx), slot(sy, sx), fp_s.at[k1, nx + ny + k2], fp_r.at[sx, sy, c], partner)
-            cp.start()
-            started.append(cp)
-    for xi in range(nx):
-        for yi in range(ny):
-            arrived(yi, xi, oc).wait_recv()
-    for xi in range(nx):
-        for yi in range(ny):
-            for ci in range(CORES):
-                o = ci * hw + yi * cw
-                out[xi * xr:(xi + 1) * xr, o:o + cw] = fin_b[xi, yi, ci].astype(BF16)
-    for cp in started:
+                emit(sy, sx, c, q)
+        for k1 in [0] + near:
+            for k2 in [0] + near:
+                sy, sx = place(k1, k2, oc)
+                landed(sy, sx, oc, q)
+                emit(sy, sx, oc, q)
+    for cp in acts + started:
         cp.wait_send()
 
 
@@ -489,13 +567,14 @@
     hw = width // CORES
     cw = hw // ny
     inner = w_gate.shape[1] // CORES
+    nq = cw // QCOLS
     steps = inner // COLS
     any_spec = pl.BlockSpec(memory_space=pl.ANY)
     dma = pltpu.SemaphoreType.DMA
     return pl.pallas_call(
         functools.partial(mlp_kernel, nx, ny),
         name='exchange_mlp',
-        out_shape=jax.ShapeDtypeStruct(hidden.shape, BF16),
+        out_shape=pltpu.VMEM(hidden.shape, BF16),
         in_specs=[any_spec] * 8,
         out_specs=pl.BlockSpec(memory_space=pltpu.VMEM),
         scratch_shapes=[
@@ -505,6 +584,7 @@
             pltpu.VMEM((w_down.shape[0], hw), BF16),
             pltpu.VMEM((xr, cw), BF16),
             pltpu.VMEM((width // LANES, LANES), BF16),
+            pltpu.VMEM((width // LANES, LANES), F32),
             pltpu.VMEM((heads, rows, dim), F32),
             pltpu.VMEM((CORES, heads, rows), F32),
             pltpu.VMEM((half_h, rows, dim), F32),
@@ -515,25 +595,27 @@
             pltpu.VMEM((nx, heads, rows), F32),
             pltpu.VMEM((nx, rows, heads), F32),
             pltpu.VMEM((CORES, xr, half_h * dim), F32),
-            pltpu.VMEM((ny, xr, cw), F32),
-            pltpu.VMEM((ny, xr, cw), F32),
-            pltpu.VMEM((CORES, ny, xr, cw), F32),
-            pltpu.VMEM((xr, width), BF16),
+            pltpu.VMEM((nq, ny, xr, QCOLS), F32),
+            pltpu.VMEM((nq, ny, xr, QCOLS), F32),
+            pltpu.VMEM((CORES, ny, nq, xr, QCOLS), F32),
+            pltpu.VMEM((CORES, ny, 8, LANES), F32),
+            pltpu.VMEM((steps, xr, COLS), F32),
+            pltpu.VMEM((steps, xr, COLS), F32),
             pltpu.VMEM((CORES, steps, xr, COLS), F32),
-            pltpu.VMEM((xr, CORES * inner), BF16),
-            pltpu.VMEM((ny, xr, cw), F32),
-            pltpu.VMEM((ny, xr, cw), F32),
-            pltpu.VMEM((nx, ny, CORES, xr, cw), F32),
+            pltpu.VMEM((CORES, xr, inner), BF16),
+            pltpu.VMEM((nq, ny, xr, QCOLS), F32),
+            pltpu.VMEM((nq, ny, xr, QCOLS), F32),
+            pltpu.VMEM((nx, ny, CORES, nq, xr, QCOLS), F32),
             dma((4,)), dma((4,)), dma((steps,)), dma((steps,)), dma((steps,)),
             dma((2,)), dma((2,)),
             dma((nx, 2)), dma((nx, 2)),
             dma((1,)), dma((1,)),
-            dma((ny,)), dma((ny,)),
-            dma((ny,)), dma((ny,)),
-            dma((ny,)), dma((ny,)),
+            dma((nq, ny)), dma((nq, ny)),
+            dma((nq, ny)), dma((CORES, ny, nq)), dma((nq, ny)),
+            dma((CORES, ny)), dma((CORES, ny)),
             dma((steps,)), dma((steps,)),
-            dma((ny,)), dma((ny,)),
-            dma((ny, 2 * nx + ny)), dma((nx, ny, CORES)),
+            dma((nq, ny)), dma((nq, ny)),
+            dma((nq, ny, 2 * nx + ny)), dma((nx, ny, CORES, nq)),
         ],
         compiler_params=pltpu.CompilerParams(vmem_limit_bytes=VMEM_LIMIT, collective_id=0, has_side_effects=True),
     )(hidden, o_part, stats, gain.reshape(width // LANES, LANES), w_o, w_gate, w_up, w_down)

time: 77.2 us -> 73.6 us (0.953)
  Pallas kernels: 74.1 us -> 71.9 us
  local copies, waits for them, and re-layouts: 2.29 us -> 0.97 us
    pallas_call x1, Pallas kernels: 56.8 us -> 54.8 us  [mlp(): pl.pallas_call(functools.partial(mlp_kernel, nx, ny), name='exchange_mlp'...]
    unnamed x1, local copies, waits for them, and re-layouts: 2.29 us -> 0.97 us
where the time goes in v3:
time: 73.6 us; the launch traced here: 73.5 us
  Pallas kernels  71.9 us (98%)
  local copies, waits for them, and re-layouts  0.97 us (1%)
    pallas_call x1, Pallas kernels, mlp(): pl.pallas_call(functools.partial(mlp_kernel, nx, ny), name='exchange_mlp'...  54.8 us
    pallas_call x1, Pallas kernels, attention(): pl.pallas_call(attn_kernel, name='block_attention', out_shape=(jax.ShapeD...  17.1 us

profile of v3, /device:TPU:97, one launch (start us, length us, event | category | flops | bytes accessed | tf_op | source)
XLA Modules:
  0.0 73.5 jit_solution(6799024212167366450)
XLA Ops:
  0.6 17.1 %block_attention.1 = (f32[1024,128]{1,0:T(8,128)}, f32[2,8,128]{2,1,0:T(8,128)}, bf16[128,2,128,128]{3,2,1,0:T(8,128)(2,1)}, bf16[128,2,128,128]{3,2,1,0:T(8,128)(2,1)}) custom-call(s32[128]{0:T(128)} %lens_in.1, bf16[128,4096]{1,0:T(8,128)(2,1)} %hid.3, bf16[32,128]{1,0:T(8,128)(2,1)} %bitcast.4, bf16[4096,1024]{1,0:T(8,128)(2,1)} %wq.1, ...), custom_call_target="tpu_custom_call" | custom-call | tf_op jit(solution)/shard_map/block_attention/pallas_call | solution.py:188
  17.7 54.8 %exchange_mlp.1 = bf16[128,4096]{1,0:T(8,128)(2,1)S(1)} custom-call(bf16[128,4096]{1,0:T(8,128)(2,1)} %hid.3, f32[8,128,128]{2,1,0:T(8,128)} %bitcast.3, f32[2,8,128]{2,1,0:T(8,128)} %get-tuple-element.8.st_in, bf16[32,128]{1,0:T(8,128)(2,1)} %bitcast.5, bf16[1024,4096]{1,0:T(8,128)(2,1)} %wo.1, bf16[4096,3584]{1,0:T(8,128)(2,1)} %wg.1, ...), custom_call_target="tpu_custom_call" | custom-call | tf_op jit(solution)/shard_map/exchange_mlp/pallas_call | solution.py:574
  72.5 1.0 %copy.17 = bf16[128,4096]{1,0:T(8,128)(2,1)} copy(bf16[128,4096]{1,0:T(8,128)(2,1)S(1)} %exchange_mlp.1) | data formatting | bytes 2097152

commit v4 on v3

--- a/solution.py
+++ b/solution.py
@@ -23,7 +23,7 @@
 
 
 def attn_kernel(lens_in, hid, gain, wq, wk, wv, kc, vc, o_out, st_out, k_out, v_out,
-                lens, obuf, hbuf, gbuf, ubuf, wbuf, qbuf, knew, vnew, kbuf, vbuf, pbuf,
+                lens, hbuf, gbuf, ubuf, wbuf, qbuf, knew, vnew, kbuf, vbuf, pbuf,
                 hsem, wsem, kin, vin, kos, vos):
     rows, groups, blk, dim = kc.shape
     heads = wq.shape[1] // dim
@@ -155,11 +155,9 @@
                 lhs.append(jnp.concatenate([jnp.where(low, ps, 0.0), jnp.where(low, 0.0, ps)], axis=1))
             vals = jnp.concatenate([vbuf[b0 + r].reshape(groups * blk, dim), vbuf[b0 + r + 1].reshape(groups * blk, dim)], axis=1)
             mix = dot32(jnp.concatenate(lhs, axis=0).astype(BF16), vals)
-            obuf[pl.ds(b0 + r, heads, stride=rows), :] = mix[:heads, :dim]
-            obuf[pl.ds(b0 + r + 1, heads, stride=rows), :] = mix[heads:, dim:]
-
-    ocopy = pltpu.make_async_copy(obuf, o_out, hsem.at[3])
-    ocopy.start()
+            o_out[pl.ds(b0 + r, heads, stride=rows), :] = mix[:heads, :dim]
+            o_out[pl.ds(b0 + r + 1, heads, stride=rows), :] = mix[heads:, dim:]
+
     half = heads // CORES
     for ci in range(CORES):
         for h in range(half):
@@ -173,7 +171,6 @@
             cp.wait()
         return 0
 
-    ocopy.wait()
     lax.fori_loop(0, nchunk, drain, 0)
 
 
@@ -188,15 +185,14 @@
     return pl.pallas_call(
         attn_kernel,
         name='block_attention',
-        out_shape=(jax.ShapeDtypeStruct((heads * rows, dim), F32),
-                   jax.ShapeDtypeStruct((CORES, heads, rows), F32),
+        out_shape=(pltpu.VMEM((heads * rows, dim), F32),
+                   pltpu.VMEM((CORES, heads, rows), F32),
                    jax.ShapeDtypeStruct(k_cache.shape, BF16),
                    jax.ShapeDtypeStruct(v_cache.shape, BF16)),
         in_specs=[any_spec] * 8,
-        out_specs=(any_spec, vm, any_spec, any_spec),
+        out_specs=(vm, vm, any_spec, any_spec),
         scratch_shapes=[
             pltpu.SMEM((rows,), jnp.int32),
-            pltpu.VMEM((heads * rows, dim), F32),
             pltpu.VMEM((rows, width), BF16),
             pltpu.VMEM((width // LANES, LANES), BF16),
             pltpu.VMEM((rows, width), BF16),
@@ -218,8 +214,8 @@
     )(seq_lens, hidden, gain.reshape(width // LANES, LANES), w_q, w_k, w_v, k_cache, v_cache)
 
 
-def mlp_kernel(nx, ny, hid, o_in, st_in, gain, wo, wg, wu, wd, out,
-               wo_b, wg_b, wu_b, wd_b, hid_b, gain_b, gf_b, o_b, st_b, po_b, pst_b, oc_b, cst_b, xo_b, xst_b, tst_b,
+def mlp_kernel(nx, ny, hid, o_b, st_b, gain, wo, wg, wu, wd, out,
+               wo_b, wg_b, wu_b, wd_b, hid_b, gain_b, gf_b, po_b, pst_b, oc_b, cst_b, xo_b, xst_b, tst_b,
                att_b, pw_b, rw_b, mid_b, ss_b, g_acc, u_acc, act_b, ab_b, pd_b, rd_b, fin_b,
                lsem, osem, gsem, usem, dsem, ds_s, ds_r, xs_s, xs_r, as_s, as_r, ws_s, ws_r, ms_s, ms_r, cs_s, ss_s, ss_r,
                dn_s, dn_r, fs_s, fs_r, fp_s, fp_r):
@@ -251,8 +247,6 @@
         return pl.ds(pl.multiple_of(i * n, n), n)
 
     loads = [
-        pltpu.make_async_copy(o_in, o_b, lsem.at[0]),
-        pltpu.make_async_copy(st_in, st_b, lsem.at[1]),
         pltpu.make_async_copy(hid.at[pl.ds(x * xr, xr), pl.ds(pl.multiple_of(c * hw + y * cw, cw), cw)], hid_b, lsem.at[2]),
         pltpu.make_async_copy(gain, gain_b, lsem.at[3]),
     ]
@@ -294,40 +288,45 @@
     for k in range(1, ny):
         pl.semaphore_signal(barrier, inc=1, device_id=peer((y + k) % ny, x), device_id_type=MESH)
         pl.semaphore_signal(barrier, inc=1, device_id=cross((y + k) % ny), device_id_type=MESH)
-    for cp in loads:
-        cp.wait()
-    gf_b[...] = gain_b[...].astype(F32)
     pl.semaphore_wait(barrier, 1 + (nx - 1) + 2 * (ny - 1))
 
-    d2d = [rcopy(o_b.at[pl.ds(half_h * oc, half_h)], po_b, ds_s.at[0], ds_r.at[0], partner),
-           rcopy(st_b.at[oc], pst_b, ds_s.at[1], ds_r.at[1], partner)]
-    for cp in d2d:
+    def head_rows(h):
+        return pl.ds(pl.multiple_of(h * rows, rows), rows)
+
+    swap = [rcopy(st_b.at[oc], pst_b, ds_s.at[half_h], ds_r.at[half_h], partner)]
+    for h in range(half_h):
+        swap.append(rcopy(o_b.at[head_rows(half_h * oc + h)], po_b.at[h], ds_s.at[h], ds_r.at[h], partner))
+    for cp in swap:
         cp.start()
     fetch_gu(1)
-    for cp in d2d:
-        cp.wait()
+    swap[0].wait_recv()
     s0 = st_b[c]
     s1 = pst_b[...]
     m0, l0, m1, l1 = s0[:half_h], s0[half_h:], s1[:half_h], s1[half_h:]
     mm = jnp.maximum(m0, m1)
     a0, a1 = jnp.exp(m0 - mm), jnp.exp(m1 - mm)
     cst_b[...] = jnp.concatenate([mm, a0 * l0 + a1 * l1], axis=0)
+
+    far_x = [2, 1, 3] if nx == 4 else list(range(1, nx))
+    sends = []
+    for k in far_x:
+        sends.append(rcopy(cst_b, xst_b.at[x], xs_s.at[k - 1, half_h], xs_r.at[x, half_h], peer(y, (x + k) % nx)))
+    for cp in sends:
+        cp.start()
     tr = jnp.concatenate([a0, a1], axis=0).T
     for h in range(half_h):
-        oc_b[h] = o_b[half_h * c + h] * tr[:, h:h + 1] + po_b[h] * tr[:, half_h + h:half_h + h + 1]
-
-    sends = []
-    for k in range(1, nx):
-        xx = (x + k) % nx
-        sends.append(rcopy(cst_b, xst_b.at[x], xs_s.at[k - 1, 0], xs_r.at[x, 0], peer(y, xx)))
-        sends.append(rcopy(oc_b.at[:, pl.ds(xx * xr, xr), :], xo_b.at[x], xs_s.at[k - 1, 1], xs_r.at[x, 1], peer(y, xx)))
-    for cp in sends:
-        cp.start()
+        swap[1 + h].wait_recv()
+        oc_b[h] = o_b[head_rows(half_h * c + h), :] * tr[:, h:h + 1] + po_b[h] * tr[:, half_h + h:half_h + h + 1]
+        for k in far_x:
+            xx = (x + k) % nx
+            cp = rcopy(oc_b.at[h, pl.ds(xx * xr, xr), :], xo_b.at[x, h], xs_s.at[k - 1, h], xs_r.at[x, h], peer(y, xx))
+            cp.start()
+            sends.append(cp)
     fetch_gu(2)
     tst_b[0] = cst_b[...].T
     for k in range(1, nx):
         xx = (x + k) % nx
-        rcopy(cst_b, xst_b.at[xx], xs_s.at[k - 1, 0], xs_r.at[xx, 0], peer(y, xx)).wait_recv()
+        rcopy(cst_b, xst_b.at[xx], xs_s.at[k - 1, half_h], xs_r.at[xx, half_h], peer(y, xx)).wait_recv()
         tst_b[k] = xst_b[xx].T
     stats = [tst_b[k, pl.ds(x * xr, xr), :] for k in range(nx)]
     mm = stats[0][:, :half_h]
@@ -337,20 +336,16 @@
     total = alphas[0] * stats[0][:, half_h:]
     for k in range(1, nx):
         total = total + alphas[k] * stats[k][:, half_h:]
-    for k in range(1, nx):
-        xx = (x + k) % nx
-        rcopy(oc_b.at[:, pl.ds(xx * xr, xr), :], xo_b.at[xx], xs_s.at[k - 1, 1], xs_r.at[xx, 1], peer(y, xx)).wait_recv()
     for h in range(half_h):
         acc = oc_b[h, pl.ds(x * xr, xr), :] * alphas[0][:, h:h + 1]
         for k in range(1, nx):
-            acc = acc + xo_b[(x + k) % nx, h] * alphas[k][:, h:h + 1]
-        att_b[c, :, h * dim:(h + 1) * dim] = (acc / total[:, h:h + 1]).astype(BF16).astype(F32)
-    swap = rcopy(att_b.at[c], att_b.at[c], as_s.at[0], as_r.at[0], partner)
-    swap.start()
-    for cp in sends:
-        cp.wait_send()
-    rcopy(att_b.at[oc], att_b.at[oc], as_s.at[0], as_r.at[0], partner).wait_recv()
-    swap.wait_send()
+            xx = (x + k) % nx
+            rcopy(oc_b.at[h, pl.ds(xx * xr, xr), :], xo_b.at[xx, h], xs_s.at[k - 1, h], xs_r.at[xx, h], peer(y, xx)).wait_recv()
+            acc = acc + xo_b[xx, h] * alphas[k][:, h:h + 1]
+        att_b[c, h] = (acc / total[:, h:h + 1]).astype(BF16).astype(F32)
+        cp = rcopy(att_b.at[c, h], att_b.at[c, h], as_s.at[h], as_r.at[h], partner)
+        cp.start()
+        sends.append(cp)
 
     def unit(yy, q):
         return pl.ds(pl.multiple_of(yy * cw + q * qw, qw), qw)
@@ -369,14 +364,29 @@
             total = total + recv_b[q, yy]
         return total
 
+    for cp in loads:
+        cp.wait()
+    gf_b[...] = gain_b[...].astype(F32)
+
     for cp in wo_loads:
         cp.wait()
-    lhs = jnp.concatenate([att_b[0], att_b[1]], axis=1).astype(BF16)
-    started = []
+    started = swap + sends
+
+    def attended(ci):
+        return jnp.concatenate([att_b[ci, h] for h in range(half_h)], axis=1).astype(BF16)
+
+    own_att = attended(c)
     for q in range(nq):
         for k in far + [0]:
             yy = (y + k) % ny
-            pw_b[q, yy] = dot32(lhs, wo_b[:, unit(yy, q)])
+            pw_b[q, yy] = dot32(own_att, wo_b[cols(c, half_h * dim), unit(yy, q)])
+    for h in range(half_h):
+        rcopy(att_b.at[oc, h], att_b.at[oc, h], as_s.at[h], as_r.at[h], partner).wait_recv()
+    other_att = attended(oc)
+    for q in range(nq):
+        for k in far + [0]:
+            yy = (y + k) % ny
+            pw_b[q, yy] = pw_b[q, yy] + dot32(other_att, wo_b[cols(oc, half_h * dim), unit(yy, q)])
             if k:
                 started.append(send_unit(pw_b, rw_b, ws_s, ws_r, q, k))
     fetch_wd(0)
@@ -507,7 +517,7 @@
 
     def spread(k1, q):
         sy, sx = place(k1, 0, c)
-        for k2 in far:
+        for k2 in far_x:
             ty, tx = place(0, k2, c)
             cp = fcopy(sy, sx, q, fp_s.at[q, k1, k2], peer(ty, tx))
             cp.start()
@@ -539,27 +549,28 @@
         emit(y, x, c, q)
         for k1 in near:
             emit(*place(k1, 0, c), c, q)
-    for q in range(nq):
-        for k1 in [0] + near:
-            for k2 in near:
-                sy, sx = place(k1, k2, c)
-                landed(sy, sx, c, q)
-                cp = fcopy(sy, sx, q, fp_s.at[q, k1, nx + ny + k2], partner)
-                cp.start()
-                started.append(cp)
-                emit(sy, sx, c, q)
-        for k1 in [0] + near:
-            for k2 in [0] + near:
-                sy, sx = place(k1, k2, oc)
-                landed(sy, sx, oc, q)
-                emit(sy, sx, oc, q)
+    order = [(k1, k2) for k1 in [0] + near for k2 in near]
+    for q in range(nq):
+        for k1, k2 in order:
+            sy, sx = place(k1, k2, c)
+            landed(sy, sx, c, q)
+            cp = fcopy(sy, sx, q, fp_s.at[q, k1, nx + ny + k2], partner)
+            cp.start()
+            started.append(cp)
+            emit(sy, sx, c, q)
+    for q in range(nq):
+        for k1, k2 in [(k1, 0) for k1 in [0] + near] + order:
+            sy, sx = place(k1, k2, oc)
+            landed(sy, sx, oc, q)
+            emit(sy, sx, oc, q)
     for cp in acts + started:
         cp.wait_send()
 
 
 def mlp(mesh, hidden, o_part, stats, gain, w_o, w_gate, w_up, w_down):
     rows, width = hidden.shape
-    heads, _, dim = o_part.shape
+    heads = stats.shape[1]
+    dim = o_part.shape[1]
     half_h = heads // CORES
     nx = mesh.shape['sp'] // CORES
     ny = mesh.shape['tp']
@@ -570,13 +581,14 @@
     nq = cw // QCOLS
     steps = inner // COLS
     any_spec = pl.BlockSpec(memory_space=pl.ANY)
+    vm = pl.BlockSpec(memory_space=pltpu.VMEM)
     dma = pltpu.SemaphoreType.DMA
     return pl.pallas_call(
         functools.partial(mlp_kernel, nx, ny),
         name='exchange_mlp',
         out_shape=pltpu.VMEM(hidden.shape, BF16),
-        in_specs=[any_spec] * 8,
-        out_specs=pl.BlockSpec(memory_space=pltpu.VMEM),
+        in_specs=[any_spec, vm, vm] + [any_spec] * 5,
+        out_specs=vm,
         scratch_shapes=[
             pltpu.VMEM((w_o.shape[0], hw), BF16),
             pltpu.VMEM((steps, width, COLS), BF16),
@@ -585,8 +597,6 @@
             pltpu.VMEM((xr, cw), BF16),
             pltpu.VMEM((width // LANES, LANES), BF16),
             pltpu.VMEM((width // LANES, LANES), F32),
-            pltpu.VMEM((heads, rows, dim), F32),
-            pltpu.VMEM((CORES, heads, rows), F32),
             pltpu.VMEM((half_h, rows, dim), F32),
             pltpu.VMEM((heads, rows), F32),
             pltpu.VMEM((half_h, rows, dim), F32),
@@ -594,7 +604,7 @@
             pltpu.VMEM((nx, half_h, xr, dim), F32),
             pltpu.VMEM((nx, heads, rows), F32),
             pltpu.VMEM((nx, rows, heads), F32),
-            pltpu.VMEM((CORES, xr, half_h * dim), F32),
+            pltpu.VMEM((CORES, half_h, xr, dim), F32),
             pltpu.VMEM((nq, ny, xr, QCOLS), F32),
             pltpu.VMEM((nq, ny, xr, QCOLS), F32),
             pltpu.VMEM((CORES, ny, nq, xr, QCOLS), F32),
@@ -607,9 +617,9 @@
             pltpu.VMEM((nq, ny, xr, QCOLS), F32),
             pltpu.VMEM((nx, ny, CORES, nq, xr, QCOLS), F32),
             dma((4,)), dma((4,)), dma((steps,)), dma((steps,)), dma((steps,)),
-            dma((2,)), dma((2,)),
-            dma((nx, 2)), dma((nx, 2)),
-            dma((1,)), dma((1,)),
+            dma((half_h + 1,)), dma((half_h + 1,)),
+            dma((nx, half_h + 1)), dma((nx, half_h + 1)),
+            dma((half_h,)), dma((half_h,)),
             dma((nq, ny)), dma((nq, ny)),
             dma((nq, ny)), dma((CORES, ny, nq)), dma((nq, ny)),
             dma((CORES, ny)), dma((CORES, ny)),
@@ -618,7 +628,7 @@
             dma((nq, ny, 2 * nx + ny)), dma((nx, ny, CORES, nq)),
         ],
         compiler_params=pltpu.CompilerParams(vmem_limit_bytes=VMEM_LIMIT, collective_id=0, has_side_effects=True),
-    )(hidden, o_part, stats, gain.reshape(width // LANES, LANES), w_o, w_gate, w_up, w_down)
+    )(hidden, pltpu.with_memory_space_constraint(o_part, pltpu.VMEM), pltpu.with_memory_space_constraint(stats, pltpu.VMEM), gain.reshape(width // LANES, LANES), w_o, w_gate, w_up, w_down)
 
 
 def solution(mesh):
@@ -630,7 +640,6 @@
 
     def local_step(hidden, seq_lens, k_cache, v_cache, attn_norm, w_q, w_k, w_v, w_o, mlp_norm, w_gate, w_up, w_down):
         o_part, stats, k_out, v_out = attention(hidden, seq_lens, k_cache, v_cache, attn_norm, w_q, w_k, w_v)
-        o_part = o_part.reshape(stats.shape[1], stats.shape[2], k_cache.shape[3])
         hidden_out = mlp(mesh, hidden, o_part, stats, mlp_norm, w_o, w_gate, w_up, w_down)
         return hidden_out, k_out, v_out
 

time: 73.6 us -> 71.2 us (0.967)
  Pallas kernels: 71.9 us -> 69.5 us
    pallas_call x1, Pallas kernels: 54.8 us -> 53.1 us  [mlp(): pl.pallas_call(functools.partial(mlp_kernel, nx, ny), name='exchange_mlp'...]
    pallas_call x1, Pallas kernels: 17.1 us -> 16.4 us  [attention(): pl.pallas_call(attn_kernel, name='block_attention', out_shape=(pltpu.VMEM...]
where the time goes in v4:
time: 71.2 us; the launch traced here: 71.1 us
  Pallas kernels  69.5 us (98%)
  local copies, waits for them, and re-layouts  0.97 us (1%)
    pallas_call x1, Pallas kernels, mlp(): pl.pallas_call(functools.partial(mlp_kernel, nx, ny), name='exchange_mlp'...  53.1 us
    pallas_call x1, Pallas kernels, attention(): pl.pallas_call(attn_kernel, name='block_attention', out_shape=(pltpu.VMEM...  16.4 us

profile of v4, /device:TPU:97, one launch (start us, length us, event | category | flops | bytes accessed | tf_op | source)
XLA Modules:
  0.0 71.1 jit_solution(9991244351815253682)
XLA Ops:
  0.6 16.4 %block_attention.1 = (f32[1024,128]{1,0:T(8,128)S(1)}, f32[2,8,128]{2,1,0:T(8,128)S(1)}, bf16[128,2,128,128]{3,2,1,0:T(8,128)(2,1)}, bf16[128,2,128,128]{3,2,1,0:T(8,128)(2,1)}) custom-call(s32[128]{0:T(128)} %lens_in.1, bf16[128,4096]{1,0:T(8,128)(2,1)} %hid.3, bf16[32,128]{1,0:T(8,128)(2,1)} %bitcast.2, bf16[4096,1024]{1,0:T(8,128)(2,1)} %wq.1, ...), custom_call_target="tpu_custom_call" | custom-call | tf_op jit(solution)/shard_map/block_attention/pallas_call | solution.py:185
  17.0 53.1 %exchange_mlp.1 = bf16[128,4096]{1,0:T(8,128)(2,1)S(1)} custom-call(bf16[128,4096]{1,0:T(8,128)(2,1)} %hid.3, f32[1024,128]{1,0:T(8,128)S(1)} %get-tuple-element.7.o_b, f32[2,8,128]{2,1,0:T(8,128)S(1)} %get-tuple-element.8.st_b, bf16[32,128]{1,0:T(8,128)(2,1)} %bitcast.3, bf16[1024,4096]{1,0:T(8,128)(2,1)} %wo.1, bf16[4096,3584]{1,0:T(8,128)(2,1)} %wg.1, ...), custom_call_target="tpu_custom_call" | custom-call | tf_op jit(solution)/shard_map/exchange_mlp/pallas_call | solution.py:586
  70.1 1.0 %copy.17 = bf16[128,4096]{1,0:T(8,128)(2,1)} copy(bf16[128,4096]{1,0:T(8,128)(2,1)S(1)} %exchange_mlp.1) | data formatting | bytes 2097152

commit v5 on v4

--- a/solution.py
+++ b/solution.py
@@ -111,7 +111,7 @@
                 vbuf[b, gi, pl.ds(t16, 16), :] = jnp.where(mask, jnp.broadcast_to(vnew[gi, pl.ds(b, 1), :], (16, dim)).astype(BF16), vt)
             return 0
 
-        lax.fori_loop(0, crow, patch, 0, unroll=4)
+        lax.fori_loop(0, crow, patch, 0, unroll=8)
         for cp in store(i):
             cp.start()
 
@@ -409,7 +409,7 @@
                 sends.append(rcopy(ss_b.at[c, y], ss_b.at[c, y], ss_s.at[0, k], ss_r.at[c, y], peer(yy, x)))
                 sends.append(rcopy(ss_b.at[c, y], ss_b.at[c, y], ss_s.at[1, k], ss_r.at[c, y], cross(yy)))
         sends.append(mid_copy(c, y, q, cs_s.at[q, 0], partner))
-        for k in far:
+        for k in near:
             sends.append(mid_copy(c, y, q, ms_s.at[q, k], peer((y + k) % ny, x)))
         for cp in sends:
             cp.start()

time: 71.2 us -> 70.8 us (level)
  no operation moved by 1% of the time
where the time goes in v5:
time: 70.8 us; the launch traced here: 70.7 us
  Pallas kernels  69.1 us (98%)
  local copies, waits for them, and re-layouts  0.97 us (1%)
    pallas_call x1, Pallas kernels, mlp(): pl.pallas_call(functools.partial(mlp_kernel, nx, ny), name='exchange_mlp'...  52.9 us
    pallas_call x1, Pallas kernels, attention(): pl.pallas_call(attn_kernel, name='block_attention', out_shape=(pltpu.VMEM...  16.2 us

profile of v5, /device:TPU:97, one launch (start us, length us, event | category | flops | bytes accessed | tf_op | source)
XLA Modules:
  0.0 70.7 jit_solution(14500843743173883503)
XLA Ops:
  0.6 16.2 %block_attention.1 = (f32[1024,128]{1,0:T(8,128)S(1)}, f32[2,8,128]{2,1,0:T(8,128)S(1)}, bf16[128,2,128,128]{3,2,1,0:T(8,128)(2,1)}, bf16[128,2,128,128]{3,2,1,0:T(8,128)(2,1)}) custom-call(s32[128]{0:T(128)} %lens_in.1, bf16[128,4096]{1,0:T(8,128)(2,1)} %hid.3, bf16[32,128]{1,0:T(8,128)(2,1)} %bitcast.2, bf16[4096,1024]{1,0:T(8,128)(2,1)} %wq.1, ...), custom_call_target="tpu_custom_call" | custom-call | tf_op jit(solution)/shard_map/block_attention/pallas_call | solution.py:185
  16.8 52.9 %exchange_mlp.1 = bf16[128,4096]{1,0:T(8,128)(2,1)S(1)} custom-call(bf16[128,4096]{1,0:T(8,128)(2,1)} %hid.3, f32[1024,128]{1,0:T(8,128)S(1)} %get-tuple-element.7.o_b, f32[2,8,128]{2,1,0:T(8,128)S(1)} %get-tuple-element.8.st_b, bf16[32,128]{1,0:T(8,128)(2,1)} %bitcast.3, bf16[1024,4096]{1,0:T(8,128)(2,1)} %wo.1, bf16[4096,3584]{1,0:T(8,128)(2,1)} %wg.1, ...), custom_call_target="tpu_custom_call" | custom-call | tf_op jit(solution)/shard_map/exchange_mlp/pallas_call | solution.py:586
  69.7 1.0 %copy.17 = bf16[128,4096]{1,0:T(8,128)(2,1)} copy(bf16[128,4096]{1,0:T(8,128)(2,1)S(1)} %exchange_mlp.1) | data formatting | bytes 2097152
